TPU v7x, 128 devices: a whole 4x4x4 slice. The times are simulated.
128 devices in a mesh: sph: 16 (over x_lo, z, core), rad: 8 (over y, x_hi).
Axes of the slice: x: 4 (x_hi: 2, x_lo: 2; x = x_hi * 2 + x_lo), y: 4, z: 4, core: 2. Of those that a mesh axis runs over, the one named last changes fastest.
Arguments:
- coeffs: bfloat16 [65536, 480], P('sph'), may hold values from -6 to 6
- interp: bfloat16 [65536, 2048], P('sph', 'rad'), may hold values from -0.055664062 to 0.055664062
- phases: float32 [64, 2048], P(None, 'rad'), may hold values from 0.3 to 3
- tables: bfloat16 [16, 480, 480], P('rad'), may hold values from -0.25 to 0.25
- bins: int32 [65536], P('sph'), may hold values from 0 to 63
Outputs:
- fields: bfloat16 [65536, 480], P('sph', 'rad')
All inputs are finite; a program needn't handle non-finite values.
Results may differ from a plain program's by a relative error of at most 0.024.
Values may be sent and summed in bfloat16 or wider, within the bound.
No kernel may reach another device: no remote copies, remote signals or barrier semaphores. Data moves between devices by JAX's collectives and lax.ppermute only.
A program may use at most 64 MiB of HBM per device.

v0:
```python
import jax
import jax.numpy as jnp
from jax import lax
from jax.sharding import PartitionSpec as P


def in_blocks(shard, dim, size):
    lengths = shard.shape
    pieces = shard.reshape(*lengths[:dim], size, lengths[dim] // size, *lengths[dim + 1 :])
    return jnp.moveaxis(pieces, dim, 0)


def summed_on_arrival(shard, axis, dim):
    pieces = in_blocks(shard, dim, lax.axis_size(axis))
    arrived = lax.all_to_all(pieces, axis, split_axis=0, concat_axis=0, tiled=True)
    return arrived.astype(jnp.float32).sum(axis=0)


def from_everyone(shard, axis):
    copies = jnp.broadcast_to(shard, (lax.axis_size(axis), *shard.shape))
    return lax.all_to_all(copies, axis, split_axis=0, concat_axis=0, tiled=True)


def in_order(pieces, dim):
    pieces = jnp.moveaxis(pieces, 0, dim)
    lengths = pieces.shape
    return pieces.reshape(*lengths[:dim], lengths[dim] * lengths[dim + 1], *lengths[dim + 2 :])


def gather_directly(shard, axis, dim):
    pieces = from_everyone(shard, axis)
    return in_order(pieces, dim)


def body(coeffs, interp, phases, tables, bins):
    node_rows = interp.shape[1]
    onehot = (bins[:, None] == jnp.arange(phases.shape[0], dtype=jnp.int32)[None, :]).astype(
        jnp.float32
    )
    lifted = jnp.dot(onehot, phases, preferred_element_type=jnp.float32)
    proj = (interp.astype(jnp.float32) * lifted).astype(jnp.bfloat16)
    partial_nodes = jnp.einsum("sr,sc->rc", proj, coeffs, preferred_element_type=jnp.float32)
    share = summed_on_arrival(partial_nodes.astype(jnp.bfloat16), "sph", 0)
    rows = share.shape[0]
    first = lax.axis_index("sph") * rows
    which = first // (node_rows // tables.shape[0])
    table = lax.dynamic_index_in_dim(tables, which, 0, keepdims=False)
    local_part = jnp.dot(
        share.astype(jnp.bfloat16), table, preferred_element_type=jnp.float32
    ).astype(jnp.bfloat16)
    angular = gather_directly(local_part, "sph", 0)
    own_spheres = lax.all_to_all(proj, "rad", split_axis=0, concat_axis=1, tiled=True)
    all_angular = gather_directly(angular, "rad", 0)
    own_fields = jnp.dot(own_spheres, all_angular, preferred_element_type=jnp.float32).astype(
        jnp.bfloat16
    )
    fields = lax.all_to_all(own_fields, "rad", split_axis=1, concat_axis=0, tiled=True)
    return fields


def solution(mesh):
    return jax.shard_map(
        body,
        mesh=mesh,
        in_specs=(P("sph", None), P("sph", "rad"), P(None, "rad"), P("rad", None, None), P("sph")),
        out_specs=P("sph", "rad"),
        check_vma=False,
    )
```

profile of v0, /device:TPU:0, one launch (start us, length us, event | category | flops | bytes accessed | tf_op | source)
XLA Modules:
  0.0 116.1 jit_solution(1360990137777865106)
XLA Ops:
  0.0 0.0 copy-start
  0.0 0.0 copy-start.1
  0.0 3.5 %fusion = bf16[4096,256]{1,0:T(8,128)(2,1)} fusion(f32[64,256]{1,0:T(8,128)} %param.7, bf16[4096,256]{1,0:T(8,128)(2,1)} %param.6, s32[4096]{0:T(1024)} %param.9), kind=kOutput, calls=%fused_computation.1 | convolution fusion | flops 137625600 | bytes 4276224 | tf_op jit(solution)/shard_map/dot_general | solution.py:40
  3.5 0.0 copy-done.1
  3.5 2.8 %convolution_convert_fusion = bf16[256,480]{0,1:T(8,128)(2,1)S(1)} fusion(bf16[4096,480]{0,1:T(8,128)(2,1)S(1)} %copy-done.1, bf16[4096,256]{1,0:T(8,128)(2,1)} %fusion), kind=kOutput, calls=%fused_computation.7 | convolution fusion | flops 1006755840 | bytes 6275072 | tf_op jit(solution)/shard_map/sr,sc->rc/dot_general | solution.py:42
  6.3 0.8 copy.10
  7.2 6.5 %all-to-all-start.1 = ((bf16[16,16,480]{2,1,0:T(8,128)(2,1)}), bf16[16,16,480]{2,1,0:T(8,128)(2,1)S(1)}, u32[]{:S(2)}, u32[]{:S(2)}) async-start(bf16[16,16,480]{2,1,0:T(8,128)(2,1)} %bitcast.2), calls=%async_computation.1 | async-start | bytes 524288 | tf_op jit(solution)/shard_map/all_to_all | solution.py:15
  13.6 8.0 %all-to-all-done.1 = bf16[16,16,480]{2,1,0:T(8,128)(2,1)S(1)} async-done(((bf16[16,16,480]{2,1,0:T(8,128)(2,1)}), bf16[16,16,480]{2,1,0:T(8,128)(2,1)S(1)}, u32[]{:S(2)}, u32[]{:S(2)}) %all-to-all-start.1) | async-done | bytes 245792 | tf_op jit(solution)/shard_map/all_to_all | solution.py:15
  21.6 0.1 reduce_sum.12
  21.7 0.0 copy-done
  21.7 0.2 convolution_convert_fusion.1
  21.9 10.6 %all_to_all.50 = bf16[16,16,480]{2,1,0:T(8,128)(2,1)S(1)} all-to-all(bf16[16,16,480]{2,1,0:T(8,128)(2,1)S(1)} %broadcast_in_dim.8), channel_id=1, replica_groups=mesh['sph'=16,'rad'=8] {'sph'}, dimensions={0} | all-to-all | bytes 491520 | tf_op jit(solution)/shard_map/all_to_all | solution.py:21
  32.5 6.6 %all-to-all-start = ((bf16[8,512,256]{2,1,0:T(8,128)(2,1)}), bf16[8,512,256]{2,1,0:T(8,128)(2,1)S(1)}, u32[]{:S(2)}, u32[]{:S(2)}) async-start(bf16[8,512,256]{2,1,0:T(8,128)(2,1)} %bitcast), calls=%async_computation | async-start | bytes 4194304 | tf_op jit(solution)/shard_map/all_to_all | solution.py:52
  39.2 0.8 copy.11
  40.0 27.4 %all-to-all-done = bf16[8,512,256]{2,1,0:T(8,128)(2,1)S(1)} async-done(((bf16[8,512,256]{2,1,0:T(8,128)(2,1)}), bf16[8,512,256]{2,1,0:T(8,128)(2,1)S(1)}, u32[]{:S(2)}, u32[]{:S(2)}) %all-to-all-start) | async-done | bytes 2097184 | tf_op jit(solution)/shard_map/all_to_all | solution.py:52
  67.4 1.1 broadcast_in_dim.9
  68.5 29.8 %all_to_all.51 = bf16[8,256,480]{1,2,0:T(8,128)(2,1)S(1)} all-to-all(bf16[8,256,480]{1,2,0:T(8,128)(2,1)S(1)} %broadcast_in_dim.9), channel_id=1, replica_groups=mesh['sph'=16,'rad'=8] {'rad'}, dimensions={0} | all-to-all | bytes 3932160 | tf_op jit(solution)/shard_map/all_to_all | solution.py:21
  98.3 2.0 %fusion.6 = bf16[512,480]{0,1:T(8,128)(2,1)} fusion(bf16[8,256,480]{1,2,0:T(8,128)(2,1)S(1)} %all_to_all.51, bf16[8,512,256]{2,1,0:T(8,128)(2,1)S(1)} %all-to-all-done), kind=kOutput, calls=%fused_computation.6 | convolution fusion | flops 1006878720 | bytes 4554752 | tf_op jit(solution)/shard_map/dot_general | solution.py:54
  100.3 1.1 all_to_all.41
  101.4 13.4 %all_to_all.52 = bf16[512,8,60]{0,2,1:T(8,128)(2,1)S(1)} all-to-all(bf16[512,8,60]{0,2,1:T(8,128)(2,1)S(1)} %all_to_all.41), channel_id=1, replica_groups=mesh['sph'=16,'rad'=8] {'rad'}, dimensions={1} | all-to-all | bytes 983040 | tf_op jit(solution)/shard_map/all_to_all | solution.py:57
  114.8 0.3 copy.15
  115.1 1.0 copy.13
  (2 shorter events, 0.1 us)
Async XLA Ops:
  0.0 21.7 %copy-start = (bf16[2,480,480]{2,1,0:T(8,128)(2,1)S(1)}, bf16[2,480,480]{2,1,0:T(8,128)(2,1)}, u32[]{:S(2)}) copy-start(bf16[2,480,480]{2,1,0:T(8,128)(2,1)} %param.8) | copy-start | bytes 2764804
  0.0 3.5 %copy-start.1 = (bf16[4096,480]{0,1:T(8,128)(2,1)S(1)}, bf16[4096,480]{0,1:T(8,128)(2,1)}, u32[]{:S(2)}) copy-start(bf16[4096,480]{0,1:T(8,128)(2,1)} %param.5) | copy-start | bytes 11796484
  7.2 14.5 %all-to-all-start.1 = ((bf16[16,16,480]{2,1,0:T(8,128)(2,1)}), bf16[16,16,480]{2,1,0:T(8,128)(2,1)S(1)}, u32[]{:S(2)}, u32[]{:S(2)}) async-start(bf16[16,16,480]{2,1,0:T(8,128)(2,1)} %bitcast.2), calls=%async_computation.1 | async-start | bytes 524288 | tf_op jit(solution)/shard_map/all_to_all | solution.py:15
  32.5 34.9 %all-to-all-start = ((bf16[8,512,256]{2,1,0:T(8,128)(2,1)}), bf16[8,512,256]{2,1,0:T(8,128)(2,1)S(1)}, u32[]{:S(2)}, u32[]{:S(2)}) async-start(bf16[8,512,256]{2,1,0:T(8,128)(2,1)} %bitcast), calls=%async_computation | async-start | bytes 4194304 | tf_op jit(solution)/shard_map/all_to_all | solution.py:52
where the time goes:
time: 117 us; the launch traced here: 116 us
  blocking collectives  53.8 us (46%)
  waiting for transfers between devices  35.4 us (30%)
  starting transfers between devices  13.1 us (11%)
  matrix products  8.47 us (7%)
  local copies, waits for them, and re-layouts  5.19 us (4%)
    all_to_all x2, blocking collectives, from_everyone(): return lax.all_to_all(copies, axis, split_axis=0, concat_axis=0, tiled=True)  40.4 us
    all_to_all x1, waiting for transfers between devices, body(): lax.all_to_all(proj, 'rad', split_axis=0, concat_axis=1, tiled=True)  27.4 us
    all_to_all x1, blocking collectives, body(): lax.all_to_all(own_fields, 'rad', split_axis=1, concat_axis=0, tiled=True)  13.4 us
    all_to_all x1, waiting for transfers between devices, summed_on_arrival(): lax.all_to_all(pieces, axis, split_axis=0, concat_axis=0, tiled=True)  8 us
    all_to_all x1, starting transfers between devices, body(): lax.all_to_all(proj, 'rad', split_axis=0, concat_axis=1, tiled=True)  6.64 us
    all_to_all x1, starting transfers between devices, summed_on_arrival(): lax.all_to_all(pieces, axis, split_axis=0, concat_axis=0, tiled=True)  6.46 us
    dot_general x1, matrix products, body(): lifted = jnp.dot(onehot, phases, preferred_element_type=jnp.float32)  3.5 us
    dot_general x1, matrix products, body(): jnp.einsum('sr,sc->rc', proj, coeffs, preferred_element_type=jnp.float32)  2.8 us
  transfers between devices with their start and end apart: 2, of which 2 were waited for; matrix products, arithmetic and copies ran while one was open for 1% of the time, Pallas kernels for 0%

commit v1 on v0

v1 whole, which is shorter than its diff:
```python
import jax
import jax.numpy as jnp
from jax import lax
from jax.experimental import pallas as pl
from jax.experimental.pallas import tpu as pltpu
from jax.sharding import Mesh
from jax.sharding import PartitionSpec as P


SWAP = [(0, 1), (1, 0)]
F32, BF16 = jnp.float32, jnp.bfloat16
HBM = pl.BlockSpec(memory_space=pltpu.HBM)
VM = pl.BlockSpec(memory_space=pltpu.VMEM)


def dot(a, b, ca, cb):
    return lax.dot_general(a, b, (((ca,), (cb,)), ((), ())), preferred_element_type=F32)


def lift_kernel(bins, phases, interp, coeffs, p0, p1, p2, p3, keep, give, iv, cv, isem, csem):
    ny = lax.axis_size("y")
    y = lax.axis_index("y")
    core = lax.axis_index("core")
    chunk = iv.shape[1]
    half = keep.shape[0]
    outs = (p0, p1, p2, p3)
    order = (1, 3, 2, 0)
    reads = []
    for n, k in enumerate(order):
        at = pl.multiple_of(((y + k) % ny) * chunk, chunk)
        ri = pltpu.make_async_copy(interp.at[pl.ds(at, chunk)], iv.at[n], isem.at[n])
        rc = pltpu.make_async_copy(coeffs.at[:, pl.ds(at, chunk)], cv.at[n], csem.at[n])
        ri.start()
        rc.start()
        reads.append((ri, rc, at))
    mine = pl.multiple_of(core * half, half)
    other = pl.multiple_of((1 - core) * half, half)
    ph = jnp.concatenate([phases[:, pl.ds(mine, half)], phases[:, pl.ds(other, half)]], axis=1)
    hi = ph.astype(BF16)
    lo = (ph - hi.astype(F32)).astype(BF16)
    both = jnp.concatenate([hi, lo], axis=0)
    nh = ph.shape[0]
    acc = jnp.zeros((cv.shape[1], 2 * half), F32)
    for n, k in enumerate(order):
        ri, rc, at = reads[n]
        b = bins[:, pl.ds(at, chunk)]
        row = lax.broadcasted_iota(jnp.int32, (nh, chunk), 0)
        one = jnp.where(row == b, 1.0, 0.0).astype(F32)
        one = jnp.concatenate([one, one], axis=0).astype(BF16)
        lifted = dot(one, both, 0, 0)
        ri.wait()
        x = jnp.concatenate([iv[n, :, pl.ds(mine, half)], iv[n, :, pl.ds(other, half)]], axis=1)
        proj = (x.astype(F32) * lifted).astype(BF16)
        outs[k][...] = proj
        rc.wait()
        acc = acc + dot(cv[n], proj, 1, 0)
    nodes = acc.T.astype(BF16)
    keep[...] = nodes[:half]
    give[...] = nodes[half:]


def lift(bins, phases, interp, coeffs_t):
    spheres, rows = interp.shape
    cols = coeffs_t.shape[0]
    chunk = spheres // 4
    piece = pltpu.VMEM((chunk, rows), BF16)
    part = pltpu.VMEM((rows // 2, cols), BF16)
    return pl.pallas_call(
        lift_kernel,
        in_specs=[VM, VM, HBM, HBM],
        out_specs=[VM] * 6,
        out_shape=[piece] * 4 + [part] * 2,
        scratch_shapes=[
            pltpu.VMEM((4, chunk, rows), BF16),
            pltpu.VMEM((4, cols, chunk), BF16),
            pltpu.SemaphoreType.DMA((4,)),
            pltpu.SemaphoreType.DMA((4,)),
        ],
        compiler_params=pltpu.CompilerParams(vmem_limit_bytes=20 << 20),
        name="lift",
    )(vmem(bins), vmem(phases), hbm(interp), hbm(coeffs_t))


def fields_kernel(mine, theirs, p0, p1, p2, p3, out):
    ny = lax.axis_size("y")
    y = lax.axis_index("y")
    acc = None
    for k, p in enumerate((p0, p1, p2, p3)):
        src = (y + ny - k) % ny
        a = jnp.concatenate([mine[src], theirs[src]], axis=0)
        f = dot(a, p[...], 0, 1)
        acc = f if acc is None else acc + f
    out[...] = acc.astype(BF16).reshape(out.shape)


def fields(mine, theirs, pieces, nrad):
    width = mine.shape[2]
    chunk = pieces[0].shape[0]
    return pl.pallas_call(
        fields_kernel,
        in_specs=[VM] * 6,
        out_specs=VM,
        out_shape=pltpu.VMEM((nrad, width // nrad, chunk), BF16),
        compiler_params=pltpu.CompilerParams(vmem_limit_bytes=16 << 20),
        name="fields",
    )(*[vmem(a) for a in (mine, theirs, *pieces)])


def finish_kernel(back, out):
    used = out.shape[0]
    chunk = back.shape[2]
    for j in range(back.shape[0] // 2):
        s = back[2 * j].astype(F32) + back[2 * j + 1].astype(F32)
        out[:, j * chunk : (j + 1) * chunk] = s[:used].astype(BF16)


def finish(back, used):
    total = back.shape[0] // 2 * back.shape[2]
    return pl.pallas_call(
        finish_kernel,
        in_specs=[VM],
        out_specs=VM,
        out_shape=jax.ShapeDtypeStruct((used, total), BF16),
        compiler_params=pltpu.CompilerParams(vmem_limit_bytes=8 << 20),
        name="finish",
    )(vmem(back))


def vmem(a):
    return pltpu.with_memory_space_constraint(a, pltpu.VMEM)


def hbm(a):
    return pltpu.with_memory_space_constraint(a, pltpu.HBM)


def exchange(pieces, axis):
    return lax.all_to_all(pieces, axis, split_axis=0, concat_axis=0, tiled=True)


def steps(coeffs, interp, phases, tables, bins):
    spheres, rows = interp.shape
    cols = coeffs.shape[1]
    ny = lax.axis_size("y")
    chips = lax.axis_size("chip")
    nrad = ny * lax.axis_size("xhi")
    core = lax.axis_index("core")
    half = rows // 2
    used = cols // nrad
    slot = -(-used // 16) * 16
    table = lax.dynamic_index_in_dim(tables, core, 0, keepdims=False)
    table = jnp.pad(table.reshape(cols, nrad, used), ((0, 0), (0, 0), (0, slot - used)))
    table = table.reshape(cols, nrad * slot)
    p0, p1, p2, p3, keep, give = lift(bins.reshape(1, spheres), phases, interp, coeffs.T)
    got = lax.ppermute(give, "core", SWAP)
    pieces = [p0] + [
        lax.ppermute(p, "y", [(i, (i + k) % ny) for i in range(ny)])
        for k, p in ((1, p1), (2, p2), (3, p3))
    ]
    chip_sum = (keep.astype(F32) + got.astype(F32)).astype(BF16)
    arrived = exchange(chip_sum.reshape(chips, half // chips, cols), "chip")
    share = arrived.astype(F32).sum(axis=0).astype(BF16)
    part = jnp.dot(share, table, preferred_element_type=F32).astype(BF16)
    mine = jnp.broadcast_to(part, (ny * chips, *part.shape))
    mine = exchange(mine, ("y", "chip"))
    mine = mine.reshape(ny, half, nrad * slot)
    theirs = lax.ppermute(mine, "core", SWAP)
    f = fields(mine, theirs, pieces, nrad)
    back = exchange(f, ("y", "xhi"))
    return finish(back, used).T


def solution(mesh):
    fine = Mesh(mesh.devices.reshape(8, 2, 4, 2), ("chip", "core", "y", "xhi"))
    sph, rad = ("chip", "core"), ("y", "xhi")
    return jax.shard_map(
        steps,
        mesh=fine,
        in_specs=(P(sph, None), P(sph, rad), P(None, rad), P(rad, None, None), P(sph)),
        out_specs=P(sph, rad),
        check_vma=False,
    )
```

time: 117 us -> 85.1 us (0.73)
  blocking collectives: 53.8 us -> 21 us
  matrix products: 8.47 us -> 0.24 us
  Pallas kernels: 0 us -> 7.87 us
  starting transfers between devices: 13.1 us -> 18.1 us
  waiting for transfers between devices: 35.4 us -> 32.1 us
    all_to_all x3 -> x1, blocking collectives: 53.8 us -> 21 us  [exchange(): return lax.all_to_all(pieces, axis, split_axis=0, concat_axis=0, tiled=True)]
    all_to_all x2, waiting for transfers between devices: 35.4 us -> 11.1 us  [exchange(): return lax.all_to_all(pieces, axis, split_axis=0, concat_axis=0, tiled=True)]
    ppermute x0 -> x5, waiting for transfers between devices: none -> 21 us  [the longest x3 19.6 us: steps(): lax.ppermute(p, 'y', [(i, (i + k) % ny) for i in range(ny)])]
    dot_general x4 -> x1, matrix products: 8.47 us -> 0.24 us  [steps(): part = jnp.dot(share, table, preferred_element_type=F32).astype(BF16)]
    pallas_call x0 -> x3, Pallas kernels: none -> 7.87 us  [the longest x1 4.63 us: lift(): pl.pallas_call(lift_kernel, in_specs=[VM, VM, HBM, HBM], out_specs=[VM] *...]
    ppermute x0 -> x5, starting transfers between devices: none -> 6.01 us  [the longest x3 6 us: steps(): lax.ppermute(p, 'y', [(i, (i + k) % ny) for i in range(ny)])]
    unnamed x6 -> x10, local copies, waits for them, and re-layouts: 1.01 us -> 3.24 us
    all_to_all x2 -> x0, local copies, waits for them, and re-layouts: 1.39 us -> none  [body(): lax.all_to_all(own_fields, 'rad', split_axis=1, concat_axis=0, tiled=True)]
  transfers between devices with their start and end apart: 2 -> 7, of which waited for: 2 -> 5; matrix products, arithmetic and copies ran while one was open for 1% -> 1% of each run, Pallas kernels for 0% -> 0%
where the time goes in v1:
time: 85.1 us; the launch traced here: 84.7 us
  waiting for transfers between devices  32.1 us (38%)
  blocking collectives  21 us (25%)
  starting transfers between devices  18.1 us (21%)
  Pallas kernels  7.87 us (9%)
  local copies, waits for them, and re-layouts  4.55 us (5%)
    all_to_all x1, blocking collectives, exchange(): return lax.all_to_all(pieces, axis, split_axis=0, concat_axis=0, tiled=True)  21 us
    ppermute x3, waiting for transfers between devices, steps(): lax.ppermute(p, 'y', [(i, (i + k) % ny) for i in range(ny)])  19.6 us
    all_to_all x2, starting transfers between devices, exchange(): return lax.all_to_all(pieces, axis, split_axis=0, concat_axis=0, tiled=True)  12.1 us
    all_to_all x2, waiting for transfers between devices, exchange(): return lax.all_to_all(pieces, axis, split_axis=0, concat_axis=0, tiled=True)  11.1 us
    ppermute x3, starting transfers between devices, steps(): lax.ppermute(p, 'y', [(i, (i + k) % ny) for i in range(ny)])  6 us
    pallas_call x1, Pallas kernels, lift(): pl.pallas_call(lift_kernel, in_specs=[VM, VM, HBM, HBM], out_specs=[VM] *...  4.63 us
    unnamed x10, local copies, waits for them, and re-layouts  3.24 us
    pallas_call x1, Pallas kernels, fields(): pl.pallas_call(fields_kernel, in_specs=[VM] * 6, out_specs=VM, out_shape=...  2.32 us
  transfers between devices with their start and end apart: 7, of which 5 were waited for; matrix products, arithmetic and copies ran while one was open for 1% of the time, Pallas kernels for 0%

profile of v1, /device:TPU:0, one launch (start us, length us, event | category | flops | bytes accessed | tf_op | source)
XLA Modules:
  0.0 84.7 jit_solution(11152106563583231581)
XLA Ops:
  0.0 0.9 %copy-done.1 = f32[64,256]{1,0:T(8,128)S(1)} copy-done((f32[64,256]{1,0:T(8,128)S(1)}, f32[64,256]{1,0:T(8,128)}, u32[]{:S(2)}) %copy-start.1) | copy-done | bytes 65560
  0.9 0.7 copy-done.2
  1.6 4.6 %lift.1 = (bf16[1024,256]{1,0:T(8,128)(2,1)S(1)}, bf16[1024,256]{1,0:T(8,128)(2,1)}, bf16[1024,256]{1,0:T(8,128)(2,1)S(1)}, bf16[1024,256]{1,0:T(8,128)(2,1)S(1)...) custom-call(s32[1,4096]{1,0:T(1,128)S(1)} %bitcast.12, f32[64,256]{1,0:T(8,128)S(1)} %copy-done.1, ...), custom_call_target="tpu_custom_call" | custom-call | tf_op jit(solution)/shard_map/lift/pallas_call | solution.py:68
  6.3 0.8 copy-done.3
  7.1 0.8 copy-done.4
  7.9 1.3 %collective-permute-done = bf16[128,480]{1,0:T(8,128)(2,1)S(1)} collective-permute-done((bf16[128,480]{1,0:T(8,128)(2,1)S(1)}, bf16[128,480]{1,0:T(8,128)(2,1)S(1)}, u32[]{:S(2)}, u32[]{:S(2)}) %collective-permute-start) | collective-permute-done | bytes 122912 | tf_op jit(solution)/shard_map/ppermute | solution.py:155
  9.2 0.7 add_convert_fusion
  9.9 6.4 %all-to-all-start = ((bf16[8,16,480]{2,1,0:T(8,128)(2,1)}), bf16[8,16,480]{2,1,0:T(8,128)(2,1)S(1)}, u32[]{:S(2)}, u32[]{:S(2)}) async-start(bf16[8,16,480]{2,1,0:T(8,128)(2,1)} %bitcast.2), calls=%async_computation | async-start | bytes 262144 | tf_op jit(solution)/shard_map/all_to_all | solution.py:138
  16.3 0.2 copy.6
  16.5 0.1 reshape.18
  16.7 0.1 pad.4
  16.7 6.1 %all-to-all-done = bf16[8,16,480]{2,1,0:T(8,128)(2,1)S(1)} async-done(((bf16[8,16,480]{2,1,0:T(8,128)(2,1)}), bf16[8,16,480]{2,1,0:T(8,128)(2,1)S(1)}, u32[]{:S(2)}, u32[]{:S(2)}) %all-to-all-start) | async-done | bytes 122912 | tf_op jit(solution)/shard_map/all_to_all | solution.py:138
  22.9 0.2 convolution_convert_fusion
  23.1 0.9 %broadcast_in_dim.3 = bf16[32,16,512]{2,1,0:T(8,128)(2,1)} broadcast(bf16[16,512]{1,0:T(8,128)(2,1)S(1)} %convolution_convert_fusion), dimensions={1,2} | broadcast | bytes 540672 | tf_op jit(solution)/shard_map/broadcast_in_dim | solution.py:164
  24.0 5.8 %all-to-all-start.1 = ((bf16[32,16,512]{2,1,0:T(8,128)(2,1)}), bf16[32,16,512]{2,1,0:T(8,128)(2,1)S(1)}, u32[]{:S(2)}, u32[]{:S(2)}) async-start(bf16[32,16,512]{2,1,0:T(8,128)(2,1)} %broadcast_in_dim.3), calls=%async_computation.1 | async-start | bytes 1048576 | tf_op jit(solution)/shard_map/all_to_all | solution.py:138
  29.8 1.9 %collective-permute-start.2 = (bf16[1024,256]{1,0:T(8,128)(2,1)}, bf16[1024,256]{1,0:T(8,128)(2,1)S(1)}, u32[]{:S(2)}, u32[]{:S(2)}) collective-permute-start(bf16[1024,256]{1,0:T(8,128)(2,1)} %get-tuple-element.14), channel_id=1, source_target_pairs={{0,2},{2,4},{4,6},{6,0},{1,3},{3,5},{5,7},{7,1},{8,10},{10,12},{12... | collective-permute-start | bytes 1572872 | tf_op jit(solution)/shard_map/ppermute | solution.py:157
  31.6 2.7 %collective-permute-start.3 = (bf16[1024,256]{1,0:T(8,128)(2,1)}, bf16[1024,256]{1,0:T(8,128)(2,1)S(1)}, u32[]{:S(2)}, u32[]{:S(2)}) collective-permute-start(bf16[1024,256]{1,0:T(8,128)(2,1)} %copy-done.4), channel_id=1, source_target_pairs={{0,4},{2,6},{4,0},{6,2},{1,5},{3,7},{5,1},{7,3},{8,12},{10,14},{12... | collective-permute-start | bytes 1572872 | tf_op jit(solution)/shard_map/ppermute | solution.py:157
  34.3 1.4 %collective-permute-start.4 = (bf16[1024,256]{1,0:T(8,128)(2,1)}, bf16[1024,256]{1,0:T(8,128)(2,1)}, u32[]{:S(2)}, u32[]{:S(2)}) collective-permute-start(bf16[1024,256]{1,0:T(8,128)(2,1)} %copy-done.3), channel_id=1, source_target_pairs={{0,6},{2,0},{4,2},{6,4},{1,7},{3,1},{5,3},{7,5},{8,14},{10,8},{12,... | collective-permute-start | bytes 1572872 | tf_op jit(solution)/shard_map/ppermute | solution.py:157
  35.8 5.0 %all-to-all-done.1 = bf16[32,16,512]{2,1,0:T(8,128)(2,1)S(1)} async-done(((bf16[32,16,512]{2,1,0:T(8,128)(2,1)}), bf16[32,16,512]{2,1,0:T(8,128)(2,1)S(1)}, u32[]{:S(2)}, u32[]{:S(2)}) %all-to-all-start.1) | async-done | bytes 524320 | tf_op jit(solution)/shard_map/all_to_all | solution.py:138
  40.7 9.4 %collective-permute-done.2.p1 = bf16[1024,256]{1,0:T(8,128)(2,1)S(1)} collective-permute-done((bf16[1024,256]{1,0:T(8,128)(2,1)}, bf16[1024,256]{1,0:T(8,128)(2,1)S(1)}, u32[]{:S(2)}, u32[]{:S(2)}) %collective-permute-start.2) | collective-permute-done | bytes 524320 | tf_op jit(solution)/shard_map/ppermute | solution.py:157
  50.2 10.2 %collective-permute-done.3.p2 = bf16[1024,256]{1,0:T(8,128)(2,1)S(1)} collective-permute-done((bf16[1024,256]{1,0:T(8,128)(2,1)}, bf16[1024,256]{1,0:T(8,128)(2,1)S(1)}, u32[]{:S(2)}, u32[]{:S(2)}) %collective-permute-start.3) | collective-permute-done | bytes 524320 | tf_op jit(solution)/shard_map/ppermute | solution.py:157
  60.4 2.3 %fields.1 = bf16[8,64,1024]{2,1,0:T(8,128)(2,1)S(1)} custom-call(bf16[4,128,512]{2,1,0:T(8,128)(2,1)S(1)} %bitcast.11, bf16[4,128,512]{2,1,0:T(8,128)(2,1)S(1)} %collective-permute-done.1.theirs, bf16[1024,256]{1,0:T(8,128)(2,1)S(1)} %get-tuple-element.13.p0, bf16[1024,256]{1,0:T(8,128)(2,1)S(1)} %collective-permute-done.2.p1, ...), custom_call_target="tpu_custom_call" | custom-call | tf_op jit(solution)/shard_map/fields/pallas_call | solution.py:99
  62.7 21.0 %all_to_all.15.back = bf16[8,64,1024]{2,1,0:T(8,128)(2,1)S(1)} all-to-all(bf16[8,64,1024]{2,1,0:T(8,128)(2,1)S(1)} %fields.1), channel_id=1, replica_groups=mesh['chip'=8,'core'=2,'y'=4,'xhi'=2] {'y','xhi'}, dimensions={0} | all-to-all | bytes 2097152 | tf_op jit(solution)/shard_map/all_to_all | solution.py:138
  83.8 0.9 %finish.1 = bf16[60,4096]{1,0:T(8,128)(2,1)} custom-call(bf16[8,64,1024]{2,1,0:T(8,128)(2,1)S(1)} %all_to_all.15.back), custom_call_target="tpu_custom_call" | custom-call | tf_op jit(solution)/shard_map/finish/pallas_call | solution.py:119
  (12 shorter events, 0.1 us)
Async XLA Ops:
  0.0 16.3 %copy-start = (bf16[2,480,480]{2,1,0:T(8,128)(2,1)S(1)}, bf16[2,480,480]{2,1,0:T(8,128)(2,1)}, u32[]{:S(2)}) copy-start(bf16[2,480,480]{2,1,0:T(8,128)(2,1)} %param.8) | copy-start | bytes 2764804
  0.0 0.9 %copy-start.1 = (f32[64,256]{1,0:T(8,128)S(1)}, f32[64,256]{1,0:T(8,128)}, u32[]{:S(2)}) copy-start(f32[64,256]{1,0:T(8,128)} %phases.1) | copy-start | bytes 196612
  0.9 0.7 copy-start.2
  6.3 0.8 copy-start.3
  7.1 0.8 copy-start.4
  7.9 1.3 %collective-permute-start = (bf16[128,480]{1,0:T(8,128)(2,1)S(1)}, bf16[128,480]{1,0:T(8,128)(2,1)S(1)}, u32[]{:S(2)}, u32[]{:S(2)}) collective-permute-start(bf16[128,480]{1,0:T(8,128)(2,1)S(1)} %get-tuple-element.12), channel_id=1, source_target_pairs={{0,8},{8,0},{1,9},{9,1},{2,10},{10,2},{3,11},{11,3},{4,12},{12,4},... | collective-permute-start | bytes 368648 | tf_op jit(solution)/shard_map/ppermute | solution.py:155
  9.9 12.9 %all-to-all-start = ((bf16[8,16,480]{2,1,0:T(8,128)(2,1)}), bf16[8,16,480]{2,1,0:T(8,128)(2,1)S(1)}, u32[]{:S(2)}, u32[]{:S(2)}) async-start(bf16[8,16,480]{2,1,0:T(8,128)(2,1)} %bitcast.2), calls=%async_computation | async-start | bytes 262144 | tf_op jit(solution)/shard_map/all_to_all | solution.py:138
  24.0 16.7 %all-to-all-start.1 = ((bf16[32,16,512]{2,1,0:T(8,128)(2,1)}), bf16[32,16,512]{2,1,0:T(8,128)(2,1)S(1)}, u32[]{:S(2)}, u32[]{:S(2)}) async-start(bf16[32,16,512]{2,1,0:T(8,128)(2,1)} %broadcast_in_dim.3), calls=%async_computation.1 | async-start | bytes 1048576 | tf_op jit(solution)/shard_map/all_to_all | solution.py:138
  29.8 20.4 %collective-permute-start.2 = (bf16[1024,256]{1,0:T(8,128)(2,1)}, bf16[1024,256]{1,0:T(8,128)(2,1)S(1)}, u32[]{:S(2)}, u32[]{:S(2)}) collective-permute-start(bf16[1024,256]{1,0:T(8,128)(2,1)} %get-tuple-element.14), channel_id=1, source_target_pairs={{0,2},{2,4},{4,6},{6,0},{1,3},{3,5},{5,7},{7,1},{8,10},{10,12},{12... | collective-permute-start | bytes 1572872 | tf_op jit(solution)/shard_map/ppermute | solution.py:157
  31.6 28.8 %collective-permute-start.3 = (bf16[1024,256]{1,0:T(8,128)(2,1)}, bf16[1024,256]{1,0:T(8,128)(2,1)S(1)}, u32[]{:S(2)}, u32[]{:S(2)}) collective-permute-start(bf16[1024,256]{1,0:T(8,128)(2,1)} %copy-done.4), channel_id=1, source_target_pairs={{0,4},{2,6},{4,0},{6,2},{1,5},{3,7},{5,1},{7,3},{8,12},{10,14},{12... | collective-permute-start | bytes 1572872 | tf_op jit(solution)/shard_map/ppermute | solution.py:157
  34.3 26.0 %collective-permute-start.4 = (bf16[1024,256]{1,0:T(8,128)(2,1)}, bf16[1024,256]{1,0:T(8,128)(2,1)}, u32[]{:S(2)}, u32[]{:S(2)}) collective-permute-start(bf16[1024,256]{1,0:T(8,128)(2,1)} %copy-done.3), channel_id=1, source_target_pairs={{0,6},{2,0},{4,2},{6,4},{1,7},{3,1},{5,3},{7,5},{8,14},{10,8},{12,... | collective-permute-start | bytes 1572872 | tf_op jit(solution)/shard_map/ppermute | solution.py:157
  40.7 19.6 %collective-permute-start.1 = (bf16[4,128,512]{2,1,0:T(8,128)(2,1)S(1)}, bf16[4,128,512]{2,1,0:T(8,128)(2,1)S(1)}, u32[]{:S(2)}, u32[]{:S(2)}) collective-permute-start(bf16[4,128,512]{2,1,0:T(8,128)(2,1)S(1)} %bitcast.10), channel_id=1, source_target_pairs={{0,8},{8,0},{1,9},{9,1},{2,10},{10,2},{3,11},{11,3},{4,12},{12,4},... | collective-permute-start | bytes 1572872 | tf_op jit(solution)/shard_map/ppermute | solution.py:167

commit v2 on v1

--- a/solution.py
+++ b/solution.py
@@ -1,3 +1,5 @@
+import functools
+
 import jax
 import jax.numpy as jnp
 from jax import lax
@@ -17,7 +19,7 @@
     return lax.dot_general(a, b, (((ca,), (cb,)), ((), ())), preferred_element_type=F32)
 
 
-def lift_kernel(bins, phases, interp, coeffs, p0, p1, p2, p3, keep, give, iv, cv, isem, csem):
+def lift_kernel(bins_h, phases_h, interp, coeffs, p0, p1, p2, p3, keep, give, bins, phases, iv, cv, pv, isem, csem, osem, ssem):
     ny = lax.axis_size("y")
     y = lax.axis_index("y")
     core = lax.axis_index("core")
@@ -25,6 +27,13 @@
     half = keep.shape[0]
     outs = (p0, p1, p2, p3)
     order = (1, 3, 2, 0)
+    writes = []
+    small = [
+        pltpu.make_async_copy(bins_h, bins, ssem.at[0]),
+        pltpu.make_async_copy(phases_h, phases, ssem.at[1]),
+    ]
+    for c in small:
+        c.start()
     reads = []
     for n, k in enumerate(order):
         at = pl.multiple_of(((y + k) % ny) * chunk, chunk)
@@ -33,6 +42,8 @@
         ri.start()
         rc.start()
         reads.append((ri, rc, at))
+    for c in small:
+        c.wait()
     mine = pl.multiple_of(core * half, half)
     other = pl.multiple_of((1 - core) * half, half)
     ph = jnp.concatenate([phases[:, pl.ds(mine, half)], phases[:, pl.ds(other, half)]], axis=1)
@@ -51,34 +62,76 @@
         ri.wait()
         x = jnp.concatenate([iv[n, :, pl.ds(mine, half)], iv[n, :, pl.ds(other, half)]], axis=1)
         proj = (x.astype(F32) * lifted).astype(BF16)
-        outs[k][...] = proj
+        if k == 0:
+            p0[...] = proj
+        else:
+            pv[n] = proj
+            w = pltpu.make_async_copy(pv.at[n], outs[k], osem.at[n])
+            w.start()
+            writes.append(w)
         rc.wait()
         acc = acc + dot(cv[n], proj, 1, 0)
     nodes = acc.T.astype(BF16)
     keep[...] = nodes[:half]
     give[...] = nodes[half:]
+    for w in writes:
+        w.wait()
 
 
 def lift(bins, phases, interp, coeffs_t):
     spheres, rows = interp.shape
     cols = coeffs_t.shape[0]
     chunk = spheres // 4
-    piece = pltpu.VMEM((chunk, rows), BF16)
+    away = pltpu.HBM((chunk, rows), BF16)
+    home = pltpu.VMEM((chunk, rows), BF16)
     part = pltpu.VMEM((rows // 2, cols), BF16)
     return pl.pallas_call(
         lift_kernel,
-        in_specs=[VM, VM, HBM, HBM],
-        out_specs=[VM] * 6,
-        out_shape=[piece] * 4 + [part] * 2,
+        in_specs=[HBM] * 4,
+        out_specs=[VM] + [HBM] * 3 + [VM] * 2,
+        out_shape=[home] + [away] * 3 + [part] * 2,
         scratch_shapes=[
+            pltpu.VMEM(bins.shape, bins.dtype),
+            pltpu.VMEM(phases.shape, phases.dtype),
             pltpu.VMEM((4, chunk, rows), BF16),
             pltpu.VMEM((4, cols, chunk), BF16),
+            pltpu.VMEM((3, chunk, rows), BF16),
             pltpu.SemaphoreType.DMA((4,)),
             pltpu.SemaphoreType.DMA((4,)),
+            pltpu.SemaphoreType.DMA((3,)),
+            pltpu.SemaphoreType.DMA((2,)),
         ],
         compiler_params=pltpu.CompilerParams(vmem_limit_bytes=20 << 20),
         name="lift",
-    )(vmem(bins), vmem(phases), hbm(interp), hbm(coeffs_t))
+    )(hbm(bins), hbm(phases), hbm(interp), hbm(coeffs_t))
+
+
+def angular_kernel(arrived, tables, out, *, nrad):
+    share = arrived[0].astype(F32)
+    for j in range(1, arrived.shape[0]):
+        share = share + arrived[j].astype(F32)
+    table = tables[lax.axis_index("core")]
+    part = dot(share.astype(BF16), table, 1, 0).astype(BF16)
+    cols = table.shape[1]
+    used, slot = cols // nrad, out.shape[2] // nrad
+    src = lax.broadcasted_iota(jnp.int32, (cols, nrad * slot), 0)
+    dst = lax.broadcasted_iota(jnp.int32, (cols, nrad * slot), 1)
+    at, within = dst // slot, dst % slot
+    pick = jnp.where((within < used) & (src == at * used + within), 1.0, 0.0).astype(BF16)
+    spread = dot(part, pick, 1, 0).astype(BF16)
+    out[...] = jnp.broadcast_to(spread[None], out.shape)
+
+
+def angular(arrived, tables, copies, nrad, slot):
+    rows = arrived.shape[1]
+    return pl.pallas_call(
+        functools.partial(angular_kernel, nrad=nrad),
+        in_specs=[VM] * 2,
+        out_specs=VM,
+        out_shape=pltpu.VMEM((copies, rows, nrad * slot), BF16),
+        compiler_params=pltpu.CompilerParams(vmem_limit_bytes=8 << 20),
+        name="angular",
+    )(vmem(arrived), vmem(tables))
 
 
 def fields_kernel(mine, theirs, p0, p1, p2, p3, out):
@@ -144,13 +197,9 @@
     ny = lax.axis_size("y")
     chips = lax.axis_size("chip")
     nrad = ny * lax.axis_size("xhi")
-    core = lax.axis_index("core")
     half = rows // 2
     used = cols // nrad
     slot = -(-used // 16) * 16
-    table = lax.dynamic_index_in_dim(tables, core, 0, keepdims=False)
-    table = jnp.pad(table.reshape(cols, nrad, used), ((0, 0), (0, 0), (0, slot - used)))
-    table = table.reshape(cols, nrad * slot)
     p0, p1, p2, p3, keep, give = lift(bins.reshape(1, spheres), phases, interp, coeffs.T)
     got = lax.ppermute(give, "core", SWAP)
     pieces = [p0] + [
@@ -159,9 +208,7 @@
     ]
     chip_sum = (keep.astype(F32) + got.astype(F32)).astype(BF16)
     arrived = exchange(chip_sum.reshape(chips, half // chips, cols), "chip")
-    share = arrived.astype(F32).sum(axis=0).astype(BF16)
-    part = jnp.dot(share, table, preferred_element_type=F32).astype(BF16)
-    mine = jnp.broadcast_to(part, (ny * chips, *part.shape))
+    mine = angular(arrived, tables, ny * chips, nrad, slot)
     mine = exchange(mine, ("y", "chip"))
     mine = mine.reshape(ny, half, nrad * slot)
     theirs = lax.ppermute(mine, "core", SWAP)

time: 85.1 us -> 81.1 us (0.953)
  blocking collectives: 21 us -> 33.7 us
  starting transfers between devices: 18.1 us -> 11.8 us
  waiting for transfers between devices: 32.1 us -> 25.9 us
  local copies, waits for them, and re-layouts: 4.55 us -> 0.01 us
  Pallas kernels: 7.87 us -> 9.27 us
    all_to_all x1 -> x2, blocking collectives: 21 us -> 33.7 us  [exchange(): return lax.all_to_all(pieces, axis, split_axis=0, concat_axis=0, tiled=True)]
    all_to_all x2 -> x1, starting transfers between devices: 12.1 us -> 5.76 us  [exchange(): return lax.all_to_all(pieces, axis, split_axis=0, concat_axis=0, tiled=True)]
    all_to_all x2 -> x1, waiting for transfers between devices: 11.1 us -> 4.97 us  [exchange(): return lax.all_to_all(pieces, axis, split_axis=0, concat_axis=0, tiled=True)]
    unnamed x10 -> x2, local copies, waits for them, and re-layouts: 3.24 us -> 0.01 us
    pallas_call x1 -> x2, Pallas kernels: 4.63 us -> 7.08 us  [the longest x1 5.87 us: lift(): pl.pallas_call(lift_kernel, in_specs=[HBM] * 4, out_specs=[VM] + [HBM] *...]
    pallas_call x1, Pallas kernels: 2.32 us -> 1.28 us  [fields(): pl.pallas_call(fields_kernel, in_specs=[VM] * 6, out_specs=VM, out_shape=...]
    broadcast_in_dim x1 -> x0, local copies, waits for them, and re-layouts: 0.89 us -> none  [steps(): mine = jnp.broadcast_to(part, (ny * chips, *part.shape))]
  transfers between devices with their start and end apart: 7 -> 6, of which waited for: 5 -> 4; matrix products, arithmetic and copies ran while one was open for 1% -> 0% of each run, Pallas kernels for 0% -> 0%
where the time goes in v2:
time: 81.1 us; the launch traced here: 80.8 us
  blocking collectives  33.7 us (42%)
  waiting for transfers between devices  25.9 us (32%)
  starting transfers between devices  11.8 us (15%)
  Pallas kernels  9.27 us (11%)
    all_to_all x2, blocking collectives, exchange(): return lax.all_to_all(pieces, axis, split_axis=0, concat_axis=0, tiled=True)  33.7 us
    ppermute x3, waiting for transfers between devices, steps(): lax.ppermute(p, 'y', [(i, (i + k) % ny) for i in range(ny)])  19.6 us
    ppermute x3, starting transfers between devices, steps(): lax.ppermute(p, 'y', [(i, (i + k) % ny) for i in range(ny)])  6 us
    pallas_call x1, Pallas kernels, lift(): pl.pallas_call(lift_kernel, in_specs=[HBM] * 4, out_specs=[VM] + [HBM] *...  5.87 us
    all_to_all x1, starting transfers between devices, exchange(): return lax.all_to_all(pieces, axis, split_axis=0, concat_axis=0, tiled=True)  5.76 us
    all_to_all x1, waiting for transfers between devices, exchange(): return lax.all_to_all(pieces, axis, split_axis=0, concat_axis=0, tiled=True)  4.97 us
  transfers between devices with their start and end apart: 6, of which 4 were waited for; matrix products, arithmetic and copies ran while one was open for 0% of the time, Pallas kernels for 0%

profile of v2, /device:TPU:0, one launch (start us, length us, event | category | flops | bytes accessed | tf_op | source)
XLA Modules:
  0.0 80.8 jit_solution(18402073888869648834)
XLA Ops:
  0.0 0.0 copy-start
  0.0 5.9 %lift.1 = (bf16[1024,256]{1,0:T(8,128)(2,1)S(1)}, bf16[1024,256]{1,0:T(8,128)(2,1)}, bf16[1024,256]{1,0:T(8,128)(2,1)}, bf16[1024,256]{1,0:T(8,128)(2,1)}, bf16[...) custom-call(s32[1,4096]{1,0:T(1,128)} %bitcast.9, f32[64,256]{1,0:T(8,128)} %phases_h.1, bf16[4096,256]{1,0:T(8,128)(2,1)} %interp.1, ...), custom_call_target="tpu_custom_call" | custom-call | tf_op jit(solution)/shard_map/lift/pallas_call | solution.py:88
  5.9 0.1 collective-permute-start
  6.0 1.3 %collective-permute-done = bf16[128,480]{1,0:T(8,128)(2,1)S(1)} collective-permute-done((bf16[128,480]{1,0:T(8,128)(2,1)S(1)}, bf16[128,480]{1,0:T(8,128)(2,1)S(1)}, u32[]{:S(2)}, u32[]{:S(2)}) %collective-permute-start) | collective-permute-done | bytes 122912 | tf_op jit(solution)/shard_map/ppermute | solution.py:204
  7.4 12.7 %all_to_all.15.arrived = bf16[8,16,480]{2,1,0:T(8,128)(2,1)S(1)} all-to-all(bf16[8,16,480]{2,1,0:T(8,128)(2,1)S(1)} %bitcast.8), channel_id=1, replica_groups=mesh['chip'=8,'core'=2,'y'=4,'xhi'=2] {'chip'}, dimensions={0} | all-to-all | bytes 245760 | tf_op jit(solution)/shard_map/all_to_all | solution.py:191
  20.1 0.0 copy-done
  20.1 1.2 %angular.1 = bf16[32,16,512]{2,1,0:T(8,128)(2,1)} custom-call(bf16[8,16,480]{2,1,0:T(8,128)(2,1)S(1)} %all_to_all.15.arrived, bf16[2,480,480]{2,1,0:T(8,128)(2,1)S(1)} %copy-done), custom_call_target="tpu_custom_call" | custom-call | tf_op jit(solution)/shard_map/angular/pallas_call | solution.py:127
  21.3 5.8 %all-to-all-start.1 = ((bf16[32,16,512]{2,1,0:T(8,128)(2,1)}), bf16[32,16,512]{2,1,0:T(8,128)(2,1)S(1)}, u32[]{:S(2)}, u32[]{:S(2)}) async-start(bf16[32,16,512]{2,1,0:T(8,128)(2,1)} %angular.1), calls=%async_computation.1 | async-start | bytes 1048576 | tf_op jit(solution)/shard_map/all_to_all | solution.py:191
  27.0 1.9 %collective-permute-start.2 = (bf16[1024,256]{1,0:T(8,128)(2,1)}, bf16[1024,256]{1,0:T(8,128)(2,1)S(1)}, u32[]{:S(2)}, u32[]{:S(2)}) collective-permute-start(bf16[1024,256]{1,0:T(8,128)(2,1)} %get-tuple-element.14), channel_id=1, source_target_pairs={{0,2},{2,4},{4,6},{6,0},{1,3},{3,5},{5,7},{7,1},{8,10},{10,12},{12... | collective-permute-start | bytes 1572872 | tf_op jit(solution)/shard_map/ppermute | solution.py:206
  28.9 2.7 %collective-permute-start.3 = (bf16[1024,256]{1,0:T(8,128)(2,1)}, bf16[1024,256]{1,0:T(8,128)(2,1)S(1)}, u32[]{:S(2)}, u32[]{:S(2)}) collective-permute-start(bf16[1024,256]{1,0:T(8,128)(2,1)} %get-tuple-element.15), channel_id=1, source_target_pairs={{0,4},{2,6},{4,0},{6,2},{1,5},{3,7},{5,1},{7,3},{8,12},{10,14},{12... | collective-permute-start | bytes 1572872 | tf_op jit(solution)/shard_map/ppermute | solution.py:206
  31.6 1.4 %collective-permute-start.4 = (bf16[1024,256]{1,0:T(8,128)(2,1)}, bf16[1024,256]{1,0:T(8,128)(2,1)S(1)}, u32[]{:S(2)}, u32[]{:S(2)}) collective-permute-start(bf16[1024,256]{1,0:T(8,128)(2,1)} %get-tuple-element.16), channel_id=1, source_target_pairs={{0,6},{2,0},{4,2},{6,4},{1,7},{3,1},{5,3},{7,5},{8,14},{10,8},{12,... | collective-permute-start | bytes 1572872 | tf_op jit(solution)/shard_map/ppermute | solution.py:206
  33.1 5.0 %all-to-all-done.1 = bf16[32,16,512]{2,1,0:T(8,128)(2,1)S(1)} async-done(((bf16[32,16,512]{2,1,0:T(8,128)(2,1)}), bf16[32,16,512]{2,1,0:T(8,128)(2,1)S(1)}, u32[]{:S(2)}, u32[]{:S(2)}) %all-to-all-start.1) | async-done | bytes 524320 | tf_op jit(solution)/shard_map/all_to_all | solution.py:191
  38.0 0.0 collective-permute-start.1
  38.0 9.4 %collective-permute-done.2.p1 = bf16[1024,256]{1,0:T(8,128)(2,1)S(1)} collective-permute-done((bf16[1024,256]{1,0:T(8,128)(2,1)}, bf16[1024,256]{1,0:T(8,128)(2,1)S(1)}, u32[]{:S(2)}, u32[]{:S(2)}) %collective-permute-start.2) | collective-permute-done | bytes 524320 | tf_op jit(solution)/shard_map/ppermute | solution.py:206
  47.4 10.2 %collective-permute-done.3.p2 = bf16[1024,256]{1,0:T(8,128)(2,1)S(1)} collective-permute-done((bf16[1024,256]{1,0:T(8,128)(2,1)}, bf16[1024,256]{1,0:T(8,128)(2,1)S(1)}, u32[]{:S(2)}, u32[]{:S(2)}) %collective-permute-start.3) | collective-permute-done | bytes 524320 | tf_op jit(solution)/shard_map/ppermute | solution.py:206
  57.7 0.0 collective-permute-done.4.p3
  57.7 0.0 collective-permute-done.1.theirs
  57.7 1.3 %fields.1 = bf16[8,64,1024]{2,1,0:T(8,128)(2,1)S(1)} custom-call(bf16[4,128,512]{2,1,0:T(8,128)(2,1)S(1)} %bitcast.6, bf16[4,128,512]{2,1,0:T(8,128)(2,1)S(1)} %collective-permute-done.1.theirs, bf16[1024,256]{1,0:T(8,128)(2,1)S(1)} %get-tuple-element.13.p0, bf16[1024,256]{1,0:T(8,128)(2,1)S(1)} %collective-permute-done.2.p1, ...), custom_call_target="tpu_custom_call" | custom-call | tf_op jit(solution)/shard_map/fields/pallas_call | solution.py:152
  59.0 20.9 %all_to_all.16.back = bf16[8,64,1024]{2,1,0:T(8,128)(2,1)S(1)} all-to-all(bf16[8,64,1024]{2,1,0:T(8,128)(2,1)S(1)} %fields.1), channel_id=1, replica_groups=mesh['chip'=8,'core'=2,'y'=4,'xhi'=2] {'y','xhi'}, dimensions={0} | all-to-all | bytes 2097152 | tf_op jit(solution)/shard_map/all_to_all | solution.py:191
  79.9 0.9 %finish.1 = bf16[60,4096]{1,0:T(8,128)(2,1)} custom-call(bf16[8,64,1024]{2,1,0:T(8,128)(2,1)S(1)} %all_to_all.16.back), custom_call_target="tpu_custom_call" | custom-call | tf_op jit(solution)/shard_map/finish/pallas_call | solution.py:172
  (1 shorter events, 0.0 us)
Async XLA Ops:
  0.0 20.1 %copy-start = (bf16[2,480,480]{2,1,0:T(8,128)(2,1)S(1)}, bf16[2,480,480]{2,1,0:T(8,128)(2,1)}, u32[]{:S(2)}) copy-start(bf16[2,480,480]{2,1,0:T(8,128)(2,1)} %tables.1) | copy-start | bytes 2764804
  5.9 1.4 %collective-permute-start = (bf16[128,480]{1,0:T(8,128)(2,1)S(1)}, bf16[128,480]{1,0:T(8,128)(2,1)S(1)}, u32[]{:S(2)}, u32[]{:S(2)}) collective-permute-start(bf16[128,480]{1,0:T(8,128)(2,1)S(1)} %get-tuple-element.12), channel_id=1, source_target_pairs={{0,8},{8,0},{1,9},{9,1},{2,10},{10,2},{3,11},{11,3},{4,12},{12,4},... | collective-permute-start | bytes 368648 | tf_op jit(solution)/shard_map/ppermute | solution.py:204
  21.3 16.7 %all-to-all-start.1 = ((bf16[32,16,512]{2,1,0:T(8,128)(2,1)}), bf16[32,16,512]{2,1,0:T(8,128)(2,1)S(1)}, u32[]{:S(2)}, u32[]{:S(2)}) async-start(bf16[32,16,512]{2,1,0:T(8,128)(2,1)} %angular.1), calls=%async_computation.1 | async-start | bytes 1048576 | tf_op jit(solution)/shard_map/all_to_all | solution.py:191
  27.0 20.4 %collective-permute-start.2 = (bf16[1024,256]{1,0:T(8,128)(2,1)}, bf16[1024,256]{1,0:T(8,128)(2,1)S(1)}, u32[]{:S(2)}, u32[]{:S(2)}) collective-permute-start(bf16[1024,256]{1,0:T(8,128)(2,1)} %get-tuple-element.14), channel_id=1, source_target_pairs={{0,2},{2,4},{4,6},{6,0},{1,3},{3,5},{5,7},{7,1},{8,10},{10,12},{12... | collective-permute-start | bytes 1572872 | tf_op jit(solution)/shard_map/ppermute | solution.py:206
  28.9 28.8 %collective-permute-start.3 = (bf16[1024,256]{1,0:T(8,128)(2,1)}, bf16[1024,256]{1,0:T(8,128)(2,1)S(1)}, u32[]{:S(2)}, u32[]{:S(2)}) collective-permute-start(bf16[1024,256]{1,0:T(8,128)(2,1)} %get-tuple-element.15), channel_id=1, source_target_pairs={{0,4},{2,6},{4,0},{6,2},{1,5},{3,7},{5,1},{7,3},{8,12},{10,14},{12... | collective-permute-start | bytes 1572872 | tf_op jit(solution)/shard_map/ppermute | solution.py:206
  31.6 26.0 %collective-permute-start.4 = (bf16[1024,256]{1,0:T(8,128)(2,1)}, bf16[1024,256]{1,0:T(8,128)(2,1)S(1)}, u32[]{:S(2)}, u32[]{:S(2)}) collective-permute-start(bf16[1024,256]{1,0:T(8,128)(2,1)} %get-tuple-element.16), channel_id=1, source_target_pairs={{0,6},{2,0},{4,2},{6,4},{1,7},{3,1},{5,3},{7,5},{8,14},{10,8},{12,... | collective-permute-start | bytes 1572872 | tf_op jit(solution)/shard_map/ppermute | solution.py:206
  38.0 19.6 %collective-permute-start.1 = (bf16[4,128,512]{2,1,0:T(8,128)(2,1)S(1)}, bf16[4,128,512]{2,1,0:T(8,128)(2,1)S(1)}, u32[]{:S(2)}, u32[]{:S(2)}) collective-permute-start(bf16[4,128,512]{2,1,0:T(8,128)(2,1)S(1)} %bitcast.5), channel_id=1, source_target_pairs={{0,8},{8,0},{1,9},{9,1},{2,10},{10,2},{3,11},{11,3},{4,12},{12,4},... | collective-permute-start | bytes 1572872 | tf_op jit(solution)/shard_map/ppermute | solution.py:214

commit v3 on v2

--- a/solution.py
+++ b/solution.py
@@ -19,15 +19,14 @@
     return lax.dot_general(a, b, (((ca,), (cb,)), ((), ())), preferred_element_type=F32)
 
 
-def lift_kernel(bins_h, phases_h, interp, coeffs, p0, p1, p2, p3, keep, give, bins, phases, iv, cv, pv, isem, csem, osem, ssem):
+def lift_kernel(bins_h, phases_h, interp, q, p1, p2, p3, bins, phases, iv, isem, osem, ssem):
     ny = lax.axis_size("y")
     y = lax.axis_index("y")
     core = lax.axis_index("core")
     chunk = iv.shape[1]
-    half = keep.shape[0]
-    outs = (p0, p1, p2, p3)
+    half = iv.shape[2] // 2
+    outs = (None, p1, p2, p3)
     order = (1, 3, 2, 0)
-    writes = []
     small = [
         pltpu.make_async_copy(bins_h, bins, ssem.at[0]),
         pltpu.make_async_copy(phases_h, phases, ssem.at[1]),
@@ -37,11 +36,9 @@
     reads = []
     for n, k in enumerate(order):
         at = pl.multiple_of(((y + k) % ny) * chunk, chunk)
-        ri = pltpu.make_async_copy(interp.at[pl.ds(at, chunk)], iv.at[n], isem.at[n])
-        rc = pltpu.make_async_copy(coeffs.at[:, pl.ds(at, chunk)], cv.at[n], csem.at[n])
-        ri.start()
-        rc.start()
-        reads.append((ri, rc, at))
+        r = pltpu.make_async_copy(interp.at[pl.ds(at, chunk)], iv.at[n], isem.at[n])
+        r.start()
+        reads.append((r, at))
     for c in small:
         c.wait()
     mine = pl.multiple_of(core * half, half)
@@ -51,59 +48,63 @@
     lo = (ph - hi.astype(F32)).astype(BF16)
     both = jnp.concatenate([hi, lo], axis=0)
     nh = ph.shape[0]
-    acc = jnp.zeros((cv.shape[1], 2 * half), F32)
+    writes = []
     for n, k in enumerate(order):
-        ri, rc, at = reads[n]
+        r, at = reads[n]
         b = bins[:, pl.ds(at, chunk)]
         row = lax.broadcasted_iota(jnp.int32, (nh, chunk), 0)
         one = jnp.where(row == b, 1.0, 0.0).astype(F32)
         one = jnp.concatenate([one, one], axis=0).astype(BF16)
         lifted = dot(one, both, 0, 0)
-        ri.wait()
+        r.wait()
         x = jnp.concatenate([iv[n, :, pl.ds(mine, half)], iv[n, :, pl.ds(other, half)]], axis=1)
-        proj = (x.astype(F32) * lifted).astype(BF16)
-        if k == 0:
-            p0[...] = proj
-        else:
-            pv[n] = proj
-            w = pltpu.make_async_copy(pv.at[n], outs[k], osem.at[n])
+        q[pl.ds(at, chunk), :] = (x.astype(F32) * lifted).astype(BF16)
+        if k:
+            w = pltpu.make_async_copy(q.at[pl.ds(at, chunk)], outs[k], osem.at[n])
             w.start()
             writes.append(w)
-        rc.wait()
-        acc = acc + dot(cv[n], proj, 1, 0)
-    nodes = acc.T.astype(BF16)
-    keep[...] = nodes[:half]
-    give[...] = nodes[half:]
     for w in writes:
         w.wait()
 
 
-def lift(bins, phases, interp, coeffs_t):
+def lift(bins, phases, interp):
     spheres, rows = interp.shape
-    cols = coeffs_t.shape[0]
     chunk = spheres // 4
-    away = pltpu.HBM((chunk, rows), BF16)
-    home = pltpu.VMEM((chunk, rows), BF16)
-    part = pltpu.VMEM((rows // 2, cols), BF16)
     return pl.pallas_call(
         lift_kernel,
-        in_specs=[HBM] * 4,
-        out_specs=[VM] + [HBM] * 3 + [VM] * 2,
-        out_shape=[home] + [away] * 3 + [part] * 2,
+        in_specs=[HBM] * 3,
+        out_specs=[VM] + [HBM] * 3,
+        out_shape=[pltpu.VMEM((spheres, rows), BF16)] + [pltpu.HBM((chunk, rows), BF16)] * 3,
         scratch_shapes=[
             pltpu.VMEM(bins.shape, bins.dtype),
             pltpu.VMEM(phases.shape, phases.dtype),
             pltpu.VMEM((4, chunk, rows), BF16),
-            pltpu.VMEM((4, cols, chunk), BF16),
-            pltpu.VMEM((3, chunk, rows), BF16),
-            pltpu.SemaphoreType.DMA((4,)),
             pltpu.SemaphoreType.DMA((4,)),
             pltpu.SemaphoreType.DMA((3,)),
             pltpu.SemaphoreType.DMA((2,)),
         ],
-        compiler_params=pltpu.CompilerParams(vmem_limit_bytes=20 << 20),
+        compiler_params=pltpu.CompilerParams(vmem_limit_bytes=12 << 20),
         name="lift",
-    )(hbm(bins), hbm(phases), hbm(interp), hbm(coeffs_t))
+    )(hbm(bins), hbm(phases), hbm(interp))
+
+
+def nodes_kernel(q, coeffs, keep, give):
+    half = keep.shape[0]
+    nodes = dot(coeffs[...], q[...], 1, 0).T.astype(BF16)
+    keep[...] = nodes[:half]
+    give[...] = nodes[half:]
+
+
+def nodes(q, coeffs_t):
+    part = pltpu.VMEM((q.shape[1] // 2, coeffs_t.shape[0]), BF16)
+    return pl.pallas_call(
+        nodes_kernel,
+        in_specs=[VM] * 2,
+        out_specs=[VM] * 2,
+        out_shape=[part] * 2,
+        compiler_params=pltpu.CompilerParams(vmem_limit_bytes=12 << 20),
+        name="nodes",
+    )(vmem(q), vmem(coeffs_t))
 
 
 def angular_kernel(arrived, tables, out, *, nrad):
@@ -134,11 +135,13 @@
     )(vmem(arrived), vmem(tables))
 
 
-def fields_kernel(mine, theirs, p0, p1, p2, p3, out):
+def fields_kernel(mine, theirs, q, p1, p2, p3, out):
     ny = lax.axis_size("y")
     y = lax.axis_index("y")
     acc = None
-    for k, p in enumerate((p0, p1, p2, p3)):
+    chunk = p1.shape[0]
+    own = q[pl.ds(pl.multiple_of(y * chunk, chunk), chunk), :]
+    for k, p in enumerate((own, p1, p2, p3)):
         src = (y + ny - k) % ny
         a = jnp.concatenate([mine[src], theirs[src]], axis=0)
         f = dot(a, p[...], 0, 1)
@@ -148,7 +151,7 @@
 
 def fields(mine, theirs, pieces, nrad):
     width = mine.shape[2]
-    chunk = pieces[0].shape[0]
+    chunk = pieces[1].shape[0]
     return pl.pallas_call(
         fields_kernel,
         in_specs=[VM] * 6,
@@ -200,9 +203,10 @@
     half = rows // 2
     used = cols // nrad
     slot = -(-used // 16) * 16
-    p0, p1, p2, p3, keep, give = lift(bins.reshape(1, spheres), phases, interp, coeffs.T)
+    q, p1, p2, p3 = lift(bins.reshape(1, spheres), phases, interp)
+    keep, give = nodes(q, coeffs.T)
     got = lax.ppermute(give, "core", SWAP)
-    pieces = [p0] + [
+    pieces = [q] + [
         lax.ppermute(p, "y", [(i, (i + k) % ny) for i in range(ny)])
         for k, p in ((1, p1), (2, p2), (3, p3))
     ]

time: 81.1 us -> 84.2 us (1.038)
  local copies, waits for them, and re-layouts: 0.01 us -> 2.11 us
    unnamed x2 -> x4, local copies, waits for them, and re-layouts: 0.01 us -> 2.11 us
    pallas_call x1, Pallas kernels: 1.28 us -> 2.48 us  [fields(): pl.pallas_call(fields_kernel, in_specs=[VM] * 6, out_specs=VM, out_shape=...]
    pallas_call x1 -> x2, Pallas kernels: 5.87 us -> 5.51 us  [the longest x1 4.25 us: lift(): pl.pallas_call(lift_kernel, in_specs=[HBM] * 3, out_specs=[VM] + [HBM] *...]
where the time goes in v3:
time: 84.2 us; the launch traced here: 83.9 us
  blocking collectives  33.7 us (40%)
  waiting for transfers between devices  26.1 us (31%)
  starting transfers between devices  11.8 us (14%)
  Pallas kernels  10.1 us (12%)
  local copies, waits for them, and re-layouts  2.11 us (3%)
    all_to_all x2, blocking collectives, exchange(): return lax.all_to_all(pieces, axis, split_axis=0, concat_axis=0, tiled=True)  33.7 us
    ppermute x3, waiting for transfers between devices, steps(): lax.ppermute(p, 'y', [(i, (i + k) % ny) for i in range(ny)])  19.7 us
    ppermute x3, starting transfers between devices, steps(): lax.ppermute(p, 'y', [(i, (i + k) % ny) for i in range(ny)])  6 us
    all_to_all x1, starting transfers between devices, exchange(): return lax.all_to_all(pieces, axis, split_axis=0, concat_axis=0, tiled=True)  5.75 us
    all_to_all x1, waiting for transfers between devices, exchange(): return lax.all_to_all(pieces, axis, split_axis=0, concat_axis=0, tiled=True)  4.97 us
    pallas_call x1, Pallas kernels, lift(): pl.pallas_call(lift_kernel, in_specs=[HBM] * 3, out_specs=[VM] + [HBM] *...  4.25 us
    pallas_call x1, Pallas kernels, fields(): pl.pallas_call(fields_kernel, in_specs=[VM] * 6, out_specs=VM, out_shape=...  2.48 us
    unnamed x4, local copies, waits for them, and re-layouts  2.11 us
  transfers between devices with their start and end apart: 6, of which 4 were waited for; matrix products, arithmetic and copies ran while one was open for 0% of the time, Pallas kernels for 0%

profile of v3, /device:TPU:0, one launch (start us, length us, event | category | flops | bytes accessed | tf_op | source)
XLA Modules:
  0.0 83.9 jit_solution(1313311379451694058)
XLA Ops:
  0.0 4.3 %lift.1 = (bf16[4096,256]{1,0:T(8,128)(2,1)S(1)}, bf16[1024,256]{1,0:T(8,128)(2,1)}, bf16[1024,256]{1,0:T(8,128)(2,1)}, bf16[1024,256]{1,0:T(8,128)(2,1)}) custom-call(s32[1,4096]{1,0:T(1,128)} %bitcast.9, f32[64,256]{1,0:T(8,128)} %phases_h.1, bf16[4096,256]{1,0:T(8,128)(2,1)} %interp.1), custom_call_target="tpu_custom_call" | custom-call | tf_op jit(solution)/shard_map/lift/pallas_call | solution.py:73
  4.3 0.0 copy-start
  4.3 2.1 %copy-done = bf16[4096,480]{0,1:T(8,128)(2,1)S(1)} copy-done((bf16[4096,480]{0,1:T(8,128)(2,1)S(1)}, bf16[4096,480]{0,1:T(8,128)(2,1)}, u32[]{:S(2)}) %copy-start) | copy-done | bytes 3932184
  6.4 0.0 copy-start.1
  6.4 1.3 %nodes.1 = (bf16[128,480]{1,0:T(8,128)(2,1)S(1)}, bf16[128,480]{1,0:T(8,128)(2,1)S(1)}) custom-call(bf16[4096,256]{1,0:T(8,128)(2,1)S(1)} %get-tuple-element.11.q, bf16[480,4096]{1,0:T(8,128)(2,1)S(1)} %bitcast.5), custom_call_target="tpu_custom_call" | custom-call | tf_op jit(solution)/shard_map/nodes/pallas_call | solution.py:100
  7.6 0.1 collective-permute-start
  7.7 1.3 %collective-permute-done = bf16[128,480]{1,0:T(8,128)(2,1)S(1)} collective-permute-done((bf16[128,480]{1,0:T(8,128)(2,1)S(1)}, bf16[128,480]{1,0:T(8,128)(2,1)S(1)}, u32[]{:S(2)}, u32[]{:S(2)}) %collective-permute-start) | collective-permute-done | bytes 122912 | tf_op jit(solution)/shard_map/ppermute | solution.py:208
  9.1 12.7 %all_to_all.15.arrived = bf16[8,16,480]{2,1,0:T(8,128)(2,1)S(1)} all-to-all(bf16[8,16,480]{2,1,0:T(8,128)(2,1)S(1)} %bitcast.8), channel_id=1, replica_groups=mesh['chip'=8,'core'=2,'y'=4,'xhi'=2] {'chip'}, dimensions={0} | all-to-all | bytes 245760 | tf_op jit(solution)/shard_map/all_to_all | solution.py:194
  21.8 0.0 copy-done.1
  21.8 1.2 %angular.1 = bf16[32,16,512]{2,1,0:T(8,128)(2,1)} custom-call(bf16[8,16,480]{2,1,0:T(8,128)(2,1)S(1)} %all_to_all.15.arrived, bf16[2,480,480]{2,1,0:T(8,128)(2,1)S(1)} %copy-done.1), custom_call_target="tpu_custom_call" | custom-call | tf_op jit(solution)/shard_map/angular/pallas_call | solution.py:128
  23.0 5.8 %all-to-all-start.1 = ((bf16[32,16,512]{2,1,0:T(8,128)(2,1)}), bf16[32,16,512]{2,1,0:T(8,128)(2,1)S(1)}, u32[]{:S(2)}, u32[]{:S(2)}) async-start(bf16[32,16,512]{2,1,0:T(8,128)(2,1)} %angular.1), calls=%async_computation.1 | async-start | bytes 1048576 | tf_op jit(solution)/shard_map/all_to_all | solution.py:194
  28.8 1.9 %collective-permute-start.2 = (bf16[1024,256]{1,0:T(8,128)(2,1)}, bf16[1024,256]{1,0:T(8,128)(2,1)S(1)}, u32[]{:S(2)}, u32[]{:S(2)}) collective-permute-start(bf16[1024,256]{1,0:T(8,128)(2,1)} %get-tuple-element.14), channel_id=1, source_target_pairs={{0,2},{2,4},{4,6},{6,0},{1,3},{3,5},{5,7},{7,1},{8,10},{10,12},{12... | collective-permute-start | bytes 1572872 | tf_op jit(solution)/shard_map/ppermute | solution.py:210
  30.7 2.7 %collective-permute-start.3 = (bf16[1024,256]{1,0:T(8,128)(2,1)}, bf16[1024,256]{1,0:T(8,128)(2,1)}, u32[]{:S(2)}, u32[]{:S(2)}) collective-permute-start(bf16[1024,256]{1,0:T(8,128)(2,1)} %get-tuple-element.15), channel_id=1, source_target_pairs={{0,4},{2,6},{4,0},{6,2},{1,5},{3,7},{5,1},{7,3},{8,12},{10,14},{12... | collective-permute-start | bytes 1572872 | tf_op jit(solution)/shard_map/ppermute | solution.py:210
  33.4 1.4 %collective-permute-start.4 = (bf16[1024,256]{1,0:T(8,128)(2,1)}, bf16[1024,256]{1,0:T(8,128)(2,1)}, u32[]{:S(2)}, u32[]{:S(2)}) collective-permute-start(bf16[1024,256]{1,0:T(8,128)(2,1)} %get-tuple-element.16), channel_id=1, source_target_pairs={{0,6},{2,0},{4,2},{6,4},{1,7},{3,1},{5,3},{7,5},{8,14},{10,8},{12,... | collective-permute-start | bytes 1572872 | tf_op jit(solution)/shard_map/ppermute | solution.py:210
  34.8 5.0 %all-to-all-done.1 = bf16[32,16,512]{2,1,0:T(8,128)(2,1)S(1)} async-done(((bf16[32,16,512]{2,1,0:T(8,128)(2,1)}), bf16[32,16,512]{2,1,0:T(8,128)(2,1)S(1)}, u32[]{:S(2)}, u32[]{:S(2)}) %all-to-all-start.1) | async-done | bytes 524320 | tf_op jit(solution)/shard_map/all_to_all | solution.py:194
  39.8 0.0 collective-permute-start.1
  39.8 9.4 %collective-permute-done.2.p1 = bf16[1024,256]{1,0:T(8,128)(2,1)S(1)} collective-permute-done((bf16[1024,256]{1,0:T(8,128)(2,1)}, bf16[1024,256]{1,0:T(8,128)(2,1)S(1)}, u32[]{:S(2)}, u32[]{:S(2)}) %collective-permute-start.2) | collective-permute-done | bytes 524320 | tf_op jit(solution)/shard_map/ppermute | solution.py:210
  49.2 10.3 %collective-permute-done.3.p2 = bf16[1024,256]{1,0:T(8,128)(2,1)} collective-permute-done((bf16[1024,256]{1,0:T(8,128)(2,1)}, bf16[1024,256]{1,0:T(8,128)(2,1)}, u32[]{:S(2)}, u32[]{:S(2)}) %collective-permute-start.3) | collective-permute-done | bytes 524320 | tf_op jit(solution)/shard_map/ppermute | solution.py:210
  59.5 0.0 collective-permute-done.4.p3
  59.5 0.0 collective-permute-done.1.theirs
  59.5 2.5 %fields.1 = bf16[8,64,1024]{2,1,0:T(8,128)(2,1)S(1)} custom-call(bf16[4,128,512]{2,1,0:T(8,128)(2,1)S(1)} %bitcast.7, bf16[4,128,512]{2,1,0:T(8,128)(2,1)S(1)} %collective-permute-done.1.theirs, bf16[4096,256]{1,0:T(8,128)(2,1)S(1)} %get-tuple-element.11.q, bf16[1024,256]{1,0:T(8,128)(2,1)S(1)} %collective-permute-done.2.p1, ...), custom_call_target="tpu_custom_call" | custom-call | tf_op jit(solution)/shard_map/fields/pallas_call | solution.py:155
  62.0 20.9 %all_to_all.16.back = bf16[8,64,1024]{2,1,0:T(8,128)(2,1)S(1)} all-to-all(bf16[8,64,1024]{2,1,0:T(8,128)(2,1)S(1)} %fields.1), channel_id=1, replica_groups=mesh['chip'=8,'core'=2,'y'=4,'xhi'=2] {'y','xhi'}, dimensions={0} | all-to-all | bytes 2097152 | tf_op jit(solution)/shard_map/all_to_all | solution.py:194
  83.0 0.9 %finish.1 = bf16[60,4096]{1,0:T(8,128)(2,1)} custom-call(bf16[8,64,1024]{2,1,0:T(8,128)(2,1)S(1)} %all_to_all.16.back), custom_call_target="tpu_custom_call" | custom-call | tf_op jit(solution)/shard_map/finish/pallas_call | solution.py:175
  (1 shorter events, 0.0 us)
Async XLA Ops:
  4.3 2.1 %copy-start = (bf16[4096,480]{0,1:T(8,128)(2,1)S(1)}, bf16[4096,480]{0,1:T(8,128)(2,1)}, u32[]{:S(2)}) copy-start(bf16[4096,480]{0,1:T(8,128)(2,1)} %param.5) | copy-start | bytes 11796484
  6.4 15.5 %copy-start.1 = (bf16[2,480,480]{2,1,0:T(8,128)(2,1)S(1)}, bf16[2,480,480]{2,1,0:T(8,128)(2,1)}, u32[]{:S(2)}) copy-start(bf16[2,480,480]{2,1,0:T(8,128)(2,1)} %tables.1) | copy-start | bytes 2764804
  7.6 1.4 %collective-permute-start = (bf16[128,480]{1,0:T(8,128)(2,1)S(1)}, bf16[128,480]{1,0:T(8,128)(2,1)S(1)}, u32[]{:S(2)}, u32[]{:S(2)}) collective-permute-start(bf16[128,480]{1,0:T(8,128)(2,1)S(1)} %get-tuple-element.13), channel_id=1, source_target_pairs={{0,8},{8,0},{1,9},{9,1},{2,10},{10,2},{3,11},{11,3},{4,12},{12,4},... | collective-permute-start | bytes 368648 | tf_op jit(solution)/shard_map/ppermute | solution.py:208
  23.0 16.7 %all-to-all-start.1 = ((bf16[32,16,512]{2,1,0:T(8,128)(2,1)}), bf16[32,16,512]{2,1,0:T(8,128)(2,1)S(1)}, u32[]{:S(2)}, u32[]{:S(2)}) async-start(bf16[32,16,512]{2,1,0:T(8,128)(2,1)} %angular.1), calls=%async_computation.1 | async-start | bytes 1048576 | tf_op jit(solution)/shard_map/all_to_all | solution.py:194
  28.8 20.4 %collective-permute-start.2 = (bf16[1024,256]{1,0:T(8,128)(2,1)}, bf16[1024,256]{1,0:T(8,128)(2,1)S(1)}, u32[]{:S(2)}, u32[]{:S(2)}) collective-permute-start(bf16[1024,256]{1,0:T(8,128)(2,1)} %get-tuple-element.14), channel_id=1, source_target_pairs={{0,2},{2,4},{4,6},{6,0},{1,3},{3,5},{5,7},{7,1},{8,10},{10,12},{12... | collective-permute-start | bytes 1572872 | tf_op jit(solution)/shard_map/ppermute | solution.py:210
  30.7 28.9 %collective-permute-start.3 = (bf16[1024,256]{1,0:T(8,128)(2,1)}, bf16[1024,256]{1,0:T(8,128)(2,1)}, u32[]{:S(2)}, u32[]{:S(2)}) collective-permute-start(bf16[1024,256]{1,0:T(8,128)(2,1)} %get-tuple-element.15), channel_id=1, source_target_pairs={{0,4},{2,6},{4,0},{6,2},{1,5},{3,7},{5,1},{7,3},{8,12},{10,14},{12... | collective-permute-start | bytes 1572872 | tf_op jit(solution)/shard_map/ppermute | solution.py:210
  33.4 26.1 %collective-permute-start.4 = (bf16[1024,256]{1,0:T(8,128)(2,1)}, bf16[1024,256]{1,0:T(8,128)(2,1)}, u32[]{:S(2)}, u32[]{:S(2)}) collective-permute-start(bf16[1024,256]{1,0:T(8,128)(2,1)} %get-tuple-element.16), channel_id=1, source_target_pairs={{0,6},{2,0},{4,2},{6,4},{1,7},{3,1},{5,3},{7,5},{8,14},{10,8},{12,... | collective-permute-start | bytes 1572872 | tf_op jit(solution)/shard_map/ppermute | solution.py:210
  39.8 19.7 %collective-permute-start.1 = (bf16[4,128,512]{2,1,0:T(8,128)(2,1)S(1)}, bf16[4,128,512]{2,1,0:T(8,128)(2,1)S(1)}, u32[]{:S(2)}, u32[]{:S(2)}) collective-permute-start(bf16[4,128,512]{2,1,0:T(8,128)(2,1)S(1)} %bitcast.6), channel_id=1, source_target_pairs={{0,8},{8,0},{1,9},{9,1},{2,10},{10,2},{3,11},{11,3},{4,12},{12,4},... | collective-permute-start | bytes 1572872 | tf_op jit(solution)/shard_map/ppermute | solution.py:218

commit v4 on v3

v4 whole, which is shorter than its diff:
```python
import functools

import jax
import jax.numpy as jnp
from jax import lax
from jax.experimental import pallas as pl
from jax.experimental.pallas import tpu as pltpu
from jax.sharding import Mesh
from jax.sharding import PartitionSpec as P


SWAP = [(0, 1), (1, 0)]
HOPS = ((0, 1), (1, 0), (3, 0), (2, 1), (1, 1), (3, 1), (2, 0), (0, 0))
F32, BF16 = jnp.float32, jnp.bfloat16
HBM = pl.BlockSpec(memory_space=pltpu.HBM)
VM = pl.BlockSpec(memory_space=pltpu.VMEM)


def dot(a, b, ca, cb):
    return lax.dot_general(a, b, (((ca,), (cb,)), ((), ())), preferred_element_type=F32)


def split_phases(phases, core):
    half = phases.shape[1] // 2
    mine = pl.multiple_of(core * half, half)
    other = pl.multiple_of((1 - core) * half, half)
    ph = jnp.concatenate([phases[:, pl.ds(mine, half)], phases[:, pl.ds(other, half)]], axis=1)
    hi = ph.astype(BF16)
    lo = (ph - hi.astype(F32)).astype(BF16)
    return jnp.concatenate([hi, lo], axis=0), mine, other


def lifted_chunk(bins, both, x_ref, mine, other, at, chunk):
    nh, half = both.shape[0] // 2, both.shape[1] // 2
    row = lax.broadcasted_iota(jnp.int32, (nh, chunk), 0)
    one = jnp.where(row == bins[:, pl.ds(at, chunk)], 1.0, 0.0)
    one = jnp.concatenate([one, one], axis=0).astype(BF16)
    lifted = dot(one, both, 0, 0)
    x = jnp.concatenate([x_ref[:, pl.ds(mine, half)], x_ref[:, pl.ds(other, half)]], axis=1)
    return (x.astype(F32) * lifted).astype(BF16)


def lift_kernel(
    bins_h, phases_h, interp, coeffs, p1, p2, p3, raw, cv, bins, phases, iv, isem, csem, ssem
):
    ny = lax.axis_size("y")
    y = lax.axis_index("y")
    core = lax.axis_index("core")
    chunk = raw.shape[0]
    small = [
        pltpu.make_async_copy(bins_h, bins, ssem.at[0]),
        pltpu.make_async_copy(phases_h, phases, ssem.at[1]),
    ]
    for c in small:
        c.start()
    reads = []
    for n, k in enumerate((1, 3, 2, 0)):
        at = pl.multiple_of(((y + k) % ny) * chunk, chunk)
        to = iv.at[n] if k else raw
        r = pltpu.make_async_copy(interp.at[pl.ds(at, chunk)], to, isem.at[n])
        r.start()
        reads.append((r, at))
    load = pltpu.make_async_copy(coeffs, cv, csem)
    load.start()
    for c in small:
        c.wait()
    both, mine, other = split_phases(phases, core)
    for n, p in enumerate((p1, p3, p2)):
        r, at = reads[n]
        r.wait()
        p[...] = lifted_chunk(bins, both, iv.at[n], mine, other, at, chunk)
    reads[3][0].wait()
    load.wait()


def lift(bins, phases, interp, coeffs_t):
    spheres, rows = interp.shape
    chunk = spheres // 4
    piece = pltpu.VMEM((chunk, rows), BF16)
    return pl.pallas_call(
        lift_kernel,
        in_specs=[HBM] * 4,
        out_specs=[VM] * 5,
        out_shape=[piece] * 4 + [pltpu.VMEM(coeffs_t.shape, BF16)],
        scratch_shapes=[
            pltpu.VMEM(bins.shape, bins.dtype),
            pltpu.VMEM(phases.shape, phases.dtype),
            pltpu.VMEM((3, chunk, rows), BF16),
            pltpu.SemaphoreType.DMA((4,)),
            pltpu.SemaphoreType.DMA(()),
            pltpu.SemaphoreType.DMA((2,)),
        ],
        compiler_params=pltpu.CompilerParams(vmem_limit_bytes=12 << 20),
        name="lift",
    )(hbm(bins), hbm(phases), hbm(interp), hbm(coeffs_t))


def nodes_kernel(bins, phases, p1, p2, p3, raw, coeffs, p0, keep, give):
    ny = lax.axis_size("y")
    y = lax.axis_index("y")
    chunk = raw.shape[0]
    half = keep.shape[0]
    both, mine, other = split_phases(phases, lax.axis_index("core"))
    acc = None
    for k, p in ((1, p1), (3, p3), (2, p2), (0, p0)):
        at = pl.multiple_of(((y + k) % ny) * chunk, chunk)
        if k == 0:
            p[...] = lifted_chunk(bins, both, raw, mine, other, at, chunk)
        part = dot(coeffs[:, pl.ds(at, chunk)], p[...], 1, 0)
        acc = part if acc is None else acc + part
    nodes = acc.T.astype(BF16)
    keep[...] = nodes[:half]
    give[...] = nodes[half:]


def nodes(bins, phases, p1, p2, p3, raw, coeffs_t):
    part = pltpu.VMEM((raw.shape[1] // 2, coeffs_t.shape[0]), BF16)
    return pl.pallas_call(
        nodes_kernel,
        in_specs=[VM] * 7,
        out_specs=[VM] * 3,
        out_shape=[pltpu.VMEM(raw.shape, BF16), part, part],
        compiler_params=pltpu.CompilerParams(vmem_limit_bytes=8 << 20),
        name="nodes",
    )(*[vmem(a) for a in (bins, phases, p1, p2, p3, raw, coeffs_t)])


def angular_kernel(arrived, tables, out, *, nrad):
    share = arrived[0].astype(F32)
    for j in range(1, arrived.shape[0]):
        share = share + arrived[j].astype(F32)
    table = tables[lax.axis_index("core")]
    part = dot(share.astype(BF16), table, 1, 0).astype(BF16)
    cols = table.shape[1]
    used, slot = cols // nrad, out.shape[2] // nrad
    src = lax.broadcasted_iota(jnp.int32, (cols, nrad * slot), 0)
    dst = lax.broadcasted_iota(jnp.int32, (cols, nrad * slot), 1)
    at, within = dst // slot, dst % slot
    pick = jnp.where((within < used) & (src == at * used + within), 1.0, 0.0).astype(BF16)
    spread = dot(part, pick, 1, 0).astype(BF16)
    out[...] = jnp.broadcast_to(spread[None], out.shape)


def angular(arrived, tables, copies, nrad, slot):
    rows = arrived.shape[1]
    return pl.pallas_call(
        functools.partial(angular_kernel, nrad=nrad),
        in_specs=[VM] * 2,
        out_specs=VM,
        out_shape=pltpu.VMEM((copies, rows, nrad * slot), BF16),
        compiler_params=pltpu.CompilerParams(vmem_limit_bytes=8 << 20),
        name="angular",
    )(vmem(arrived), vmem(tables))


def fields_kernel(mine, theirs, p0, p1, p2, p3, *refs):
    outs, f_ref = refs[:-1], refs[-1]
    ny, nx = lax.axis_size("y"), lax.axis_size("xhi")
    y, x = lax.axis_index("y"), lax.axis_index("xhi")
    acc = None
    for k, p in enumerate((p0, p1, p2, p3)):
        src = (y + ny - k) % ny
        a = jnp.concatenate([mine[src], theirs[src]], axis=0)
        f = dot(a, p[...], 0, 1)
        acc = f if acc is None else acc + f
    f_ref[...] = acc.astype(BF16).reshape(f_ref.shape)
    for (dy, dx), out in zip(HOPS, outs):
        out[...] = f_ref[(y + dy) % ny * nx + (x + dx) % nx]


def fields(mine, theirs, pieces, nrad):
    slot = mine.shape[2] // nrad
    chunk = pieces[0].shape[0]
    return pl.pallas_call(
        fields_kernel,
        in_specs=[VM] * 6,
        out_specs=[VM] * nrad,
        out_shape=[pltpu.VMEM((slot, chunk), BF16)] * nrad,
        scratch_shapes=[pltpu.VMEM((nrad, slot, chunk), BF16)],
        compiler_params=pltpu.CompilerParams(vmem_limit_bytes=8 << 20),
        name="fields",
    )(*[vmem(a) for a in (mine, theirs, *pieces)])


def finish_kernel(*refs):
    back, out = dict(zip(HOPS, refs[:-1])), refs[-1]
    ny = lax.axis_size("y")
    y = lax.axis_index("y")
    used = out.shape[0]
    chunk = refs[0].shape[1]
    for dy in range(4):
        s = back[dy, 0][...].astype(F32) + back[dy, 1][...].astype(F32)
        at = pl.multiple_of((y + ny - dy) % ny * chunk, chunk)
        out[:, pl.ds(at, chunk)] = s[:used].astype(BF16)


def finish(back, used):
    total = 4 * back[0].shape[1]
    return pl.pallas_call(
        finish_kernel,
        in_specs=[VM] * len(back),
        out_specs=VM,
        out_shape=jax.ShapeDtypeStruct((used, total), BF16),
        compiler_params=pltpu.CompilerParams(vmem_limit_bytes=8 << 20),
        name="finish",
    )(*[vmem(a) for a in back])


def deliver(piece, dy, dx):
    ny, nx = lax.axis_size("y"), lax.axis_size("xhi")
    if (dy, dx) == (0, 0):
        return piece
    hops = [
        (y * nx + x, (y + dy) % ny * nx + (x + dx) % nx) for y in range(ny) for x in range(nx)
    ]
    return lax.ppermute(piece, ("y", "xhi"), hops)


def vmem(a):
    return pltpu.with_memory_space_constraint(a, pltpu.VMEM)


def hbm(a):
    return pltpu.with_memory_space_constraint(a, pltpu.HBM)


def exchange(pieces, axis):
    return lax.all_to_all(pieces, axis, split_axis=0, concat_axis=0, tiled=True)


def steps(coeffs, interp, phases, tables, bins):
    spheres, rows = interp.shape
    cols = coeffs.shape[1]
    ny = lax.axis_size("y")
    chips = lax.axis_size("chip")
    nrad = ny * lax.axis_size("xhi")
    half = rows // 2
    used = cols // nrad
    slot = -(-used // 16) * 16
    bins = bins.reshape(1, spheres)
    p1, p2, p3, raw, coeffs_t = lift(bins, phases, interp, coeffs.T)
    p0, keep, give = nodes(bins, phases, p1, p2, p3, raw, coeffs_t)
    got = lax.ppermute(give, "core", SWAP)
    pieces = [p0] + [
        lax.ppermute(p, "y", [(i, (i + k) % ny) for i in range(ny)])
        for k, p in ((1, p1), (2, p2), (3, p3))
    ]
    chip_sum = (keep.astype(F32) + got.astype(F32)).astype(BF16)
    arrived = exchange(chip_sum.reshape(chips, half // chips, cols), "chip")
    mine = angular(arrived, tables, ny * chips, nrad, slot)
    mine = exchange(mine, ("y", "chip"))
    mine = mine.reshape(ny, half, nrad * slot)
    theirs = lax.ppermute(mine, "core", SWAP)
    f = fields(mine, theirs, pieces, nrad)
    back = [deliver(piece, dy, dx) for (dy, dx), piece in zip(HOPS, f)]
    return finish(back, used).T


def solution(mesh):
    fine = Mesh(mesh.devices.reshape(8, 2, 4, 2), ("chip", "core", "y", "xhi"))
    sph, rad = ("chip", "core"), ("y", "xhi")
    return jax.shard_map(
        steps,
        mesh=fine,
        in_specs=(P(sph, None), P(sph, rad), P(None, rad), P(rad, None, None), P(sph)),
        out_specs=P(sph, rad),
        check_vma=False,
    )
```

time: 84.2 us -> 79.3 us (0.942)
  blocking collectives: 33.7 us -> 12.7 us
  starting transfers between devices: 11.8 us -> 26.1 us
  waiting for transfers between devices: 26.1 us -> 31 us
  local copies, waits for them, and re-layouts: 2.11 us -> 0.01 us
  Pallas kernels: 10.1 us -> 9.08 us
    all_to_all x2 -> x1, blocking collectives: 33.7 us -> 12.7 us  [exchange(): return lax.all_to_all(pieces, axis, split_axis=0, concat_axis=0, tiled=True)]
    ppermute x0 -> x7, starting transfers between devices: none -> 14.2 us  [deliver(): return lax.ppermute(piece, ('y', 'xhi'), hops)]
    ppermute x0 -> x7, waiting for transfers between devices: none -> 4.97 us  [deliver(): return lax.ppermute(piece, ('y', 'xhi'), hops)]
    unnamed x4 -> x6, local copies, waits for them, and re-layouts: 2.11 us -> 0.01 us
    pallas_call x4, Pallas kernels: 8.9 us -> 7.89 us  [the longest x1 2.8 us: lift(): pl.pallas_call(lift_kernel, in_specs=[HBM] * 4, out_specs=[VM] * 5, out_s...]
  transfers between devices with their start and end apart: 6 -> 13, of which waited for: 4 -> 8; matrix products, arithmetic and copies ran while one was open for 0% -> 0% of each run, Pallas kernels for 0% -> 0%
where the time goes in v4:
time: 79.3 us; the launch traced here: 79 us
  waiting for transfers between devices  31 us (39%)
  starting transfers between devices  26.1 us (33%)
  blocking collectives  12.7 us (16%)
  Pallas kernels  9.08 us (11%)
    ppermute x3, waiting for transfers between devices, steps(): lax.ppermute(p, 'y', [(i, (i + k) % ny) for i in range(ny)])  19.7 us
    ppermute x7, starting transfers between devices, deliver(): return lax.ppermute(piece, ('y', 'xhi'), hops)  14.2 us
    all_to_all x1, blocking collectives, exchange(): return lax.all_to_all(pieces, axis, split_axis=0, concat_axis=0, tiled=True)  12.7 us
    ppermute x3, starting transfers between devices, steps(): lax.ppermute(p, 'y', [(i, (i + k) % ny) for i in range(ny)])  6 us
    all_to_all x1, starting transfers between devices, exchange(): return lax.all_to_all(pieces, axis, split_axis=0, concat_axis=0, tiled=True)  5.76 us
    all_to_all x1, waiting for transfers between devices, exchange(): return lax.all_to_all(pieces, axis, split_axis=0, concat_axis=0, tiled=True)  4.97 us
    ppermute x7, waiting for transfers between devices, deliver(): return lax.ppermute(piece, ('y', 'xhi'), hops)  4.97 us
    pallas_call x1, Pallas kernels, lift(): pl.pallas_call(lift_kernel, in_specs=[HBM] * 4, out_specs=[VM] * 5, out_s...  2.8 us
  transfers between devices with their start and end apart: 13, of which 8 were waited for; matrix products, arithmetic and copies ran while one was open for 0% of the time, Pallas kernels for 0%

profile of v4, /device:TPU:0, one launch (start us, length us, event | category | flops | bytes accessed | tf_op | source)
XLA Modules:
  0.0 79.0 jit_solution(6421360821877242425)
XLA Ops:
  0.0 2.8 %lift.1 = (bf16[1024,256]{1,0:T(8,128)(2,1)S(1)}, bf16[1024,256]{1,0:T(8,128)(2,1)S(1)}, bf16[1024,256]{1,0:T(8,128)(2,1)S(1)}, bf16[1024,256]{1,0:T(8,128)(2,1)S(1)}, bf16[480,4096]{1,0:T(8,128)(2,1)S(1)}) custom-call(s32[1,4096]{1,0:T(1,128)} %bitcast.7, f32[64,256]{1,0:T(8,128)} %phases.1, bf16[4096,256]{1,0:T(8,128)(2,1)} %interp.1, ...), custom_call_target="tpu_custom_call" | custom-call | tf_op jit(solution)/shard_map/lift/pallas_call | solution.py:80
  2.8 1.6 %nodes.1 = (bf16[1024,256]{1,0:T(8,128)(2,1)S(1)}, bf16[128,480]{1,0:T(8,128)(2,1)S(1)}, bf16[128,480]{1,0:T(8,128)(2,1)S(1)}) custom-call(s32[1,4096]{1,0:T(1,128)S(1)} %bitcast.8, f32[64,256]{1,0:T(8,128)S(1)} %copy-done.1, bf16[1024,256]{1,0:T(8,128)(2,1)S(1)} %get-tuple-element.21.p1, bf16[1024,256]{1,0:T(8,128)(2,1)S(1)} %get-tuple-element.22.p2, ...), custom_call_target="tpu_custom_call" | custom-call | tf_op jit(solution)/shard_map/nodes/pallas_call | solution.py:118
  4.6 1.3 %collective-permute-done = bf16[128,480]{1,0:T(8,128)(2,1)S(1)} collective-permute-done((bf16[128,480]{1,0:T(8,128)(2,1)S(1)}, bf16[128,480]{1,0:T(8,128)(2,1)S(1)}, u32[]{:S(2)}, u32[]{:S(2)}) %collective-permute-start) | collective-permute-done | bytes 122912 | tf_op jit(solution)/shard_map/ppermute | solution.py:243
  5.9 12.7 %all_to_all.10.arrived = bf16[8,16,480]{2,1,0:T(8,128)(2,1)S(1)} all-to-all(bf16[8,16,480]{2,1,0:T(8,128)(2,1)S(1)} %bitcast.10), channel_id=1, replica_groups=mesh['chip'=8,'core'=2,'y'=4,'xhi'=2] {'chip'}, dimensions={0} | all-to-all | bytes 245760 | tf_op jit(solution)/shard_map/all_to_all | solution.py:228
  18.7 1.2 %angular.1 = bf16[32,16,512]{2,1,0:T(8,128)(2,1)} custom-call(bf16[8,16,480]{2,1,0:T(8,128)(2,1)S(1)} %all_to_all.10.arrived, bf16[2,480,480]{2,1,0:T(8,128)(2,1)S(1)} %copy-done), custom_call_target="tpu_custom_call" | custom-call | tf_op jit(solution)/shard_map/angular/pallas_call | solution.py:146
  19.9 5.8 %all-to-all-start.1 = ((bf16[32,16,512]{2,1,0:T(8,128)(2,1)}), bf16[32,16,512]{2,1,0:T(8,128)(2,1)S(1)}, u32[]{:S(2)}, u32[]{:S(2)}) async-start(bf16[32,16,512]{2,1,0:T(8,128)(2,1)} %angular.1), calls=%async_computation.1 | async-start | bytes 1048576 | tf_op jit(solution)/shard_map/all_to_all | solution.py:228
  25.6 1.9 %collective-permute-start.2 = (bf16[1024,256]{1,0:T(8,128)(2,1)S(1)}, bf16[1024,256]{1,0:T(8,128)(2,1)S(1)}, u32[]{:S(2)}, u32[]{:S(2)}) collective-permute-start(bf16[1024,256]{1,0:T(8,128)(2,1)S(1)} %get-tuple-element.21.p1), channel_id=1, source_target_pairs={{0,2},{2,4},{4,6},{6,0},{1,3},{3,5},{5,7},{7,1},{8,10},{10,12},{12... | collective-permute-start | bytes 1572872 | tf_op jit(solution)/shard_map/ppermute | solution.py:245
  27.5 2.7 %collective-permute-start.3 = (bf16[1024,256]{1,0:T(8,128)(2,1)S(1)}, bf16[1024,256]{1,0:T(8,128)(2,1)}, u32[]{:S(2)}, u32[]{:S(2)}) collective-permute-start(bf16[1024,256]{1,0:T(8,128)(2,1)S(1)} %get-tuple-element.22.p2), channel_id=1, source_target_pairs={{0,4},{2,6},{4,0},{6,2},{1,5},{3,7},{5,1},{7,3},{8,12},{10,14},{12... | collective-permute-start | bytes 1572872 | tf_op jit(solution)/shard_map/ppermute | solution.py:245
  30.2 1.4 %collective-permute-start.4 = (bf16[1024,256]{1,0:T(8,128)(2,1)S(1)}, bf16[1024,256]{1,0:T(8,128)(2,1)}, u32[]{:S(2)}, u32[]{:S(2)}) collective-permute-start(bf16[1024,256]{1,0:T(8,128)(2,1)S(1)} %get-tuple-element.23.p3), channel_id=1, source_target_pairs={{0,6},{2,0},{4,2},{6,4},{1,7},{3,1},{5,3},{7,5},{8,14},{10,8},{12,... | collective-permute-start | bytes 1572872 | tf_op jit(solution)/shard_map/ppermute | solution.py:245
  31.6 5.0 %all-to-all-done.1 = bf16[32,16,512]{2,1,0:T(8,128)(2,1)S(1)} async-done(((bf16[32,16,512]{2,1,0:T(8,128)(2,1)}), bf16[32,16,512]{2,1,0:T(8,128)(2,1)S(1)}, u32[]{:S(2)}, u32[]{:S(2)}) %all-to-all-start.1) | async-done | bytes 524320 | tf_op jit(solution)/shard_map/all_to_all | solution.py:228
  36.6 9.4 %collective-permute-done.2.p1 = bf16[1024,256]{1,0:T(8,128)(2,1)S(1)} collective-permute-done((bf16[1024,256]{1,0:T(8,128)(2,1)S(1)}, bf16[1024,256]{1,0:T(8,128)(2,1)S(1)}, u32[]{:S(2)}, u32[]{:S(2)}) %collective-permute-start.2) | collective-permute-done | bytes 524320 | tf_op jit(solution)/shard_map/ppermute | solution.py:245
  46.0 10.3 %collective-permute-done.3.p2 = bf16[1024,256]{1,0:T(8,128)(2,1)} collective-permute-done((bf16[1024,256]{1,0:T(8,128)(2,1)S(1)}, bf16[1024,256]{1,0:T(8,128)(2,1)}, u32[]{:S(2)}, u32[]{:S(2)}) %collective-permute-start.3) | collective-permute-done | bytes 524320 | tf_op jit(solution)/shard_map/ppermute | solution.py:245
  56.3 2.6 %fields.1 = (bf16[64,1024]{1,0:T(8,128)(2,1)S(1)}, bf16[64,1024]{1,0:T(8,128)(2,1)S(1)}, bf16[64,1024]{1,0:T(8,128)(2,1)S(1)}, bf16[64,1024]{1,0:T(8,128)(2,1)S(...) custom-call(bf16[4,128,512]{2,1,0:T(8,128)(2,1)S(1)} %bitcast.6, ...), custom_call_target="tpu_custom_call" | custom-call | tf_op jit(solution)/shard_map/fields/pallas_call | solution.py:174
  58.9 2.8 %collective-permute-start.5 = (bf16[64,1024]{1,0:T(8,128)(2,1)S(1)}, bf16[64,1024]{1,0:T(8,128)(2,1)S(1)}, u32[]{:S(2)}, u32[]{:S(2)}) collective-permute-start(bf16[64,1024]{1,0:T(8,128)(2,1)S(1)} %get-tuple-element.29), channel_id=1, source_target_pairs={{0,1},{1,0},{2,3},{3,2},{4,5},{5,4},{6,7},{7,6},{8,9},{9,8},{10,11... | collective-permute-start | bytes 393224 | tf_op jit(solution)/shard_map/ppermute | solution.py:216
  61.7 0.5 collective-permute-start.6
  62.2 2.7 %collective-permute-start.7 = (bf16[64,1024]{1,0:T(8,128)(2,1)S(1)}, bf16[64,1024]{1,0:T(8,128)(2,1)S(1)}, u32[]{:S(2)}, u32[]{:S(2)}) collective-permute-start(bf16[64,1024]{1,0:T(8,128)(2,1)S(1)} %get-tuple-element.31), channel_id=1, source_target_pairs={{0,6},{1,7},{2,0},{3,1},{4,2},{5,3},{6,4},{7,5},{8,14},{9,15},{10,... | collective-permute-start | bytes 393224 | tf_op jit(solution)/shard_map/ppermute | solution.py:216
  65.0 0.6 collective-permute-start.8
  65.6 2.7 %collective-permute-start.9 = (bf16[64,1024]{1,0:T(8,128)(2,1)S(1)}, bf16[64,1024]{1,0:T(8,128)(2,1)S(1)}, u32[]{:S(2)}, u32[]{:S(2)}) collective-permute-start(bf16[64,1024]{1,0:T(8,128)(2,1)S(1)} %get-tuple-element.33), channel_id=1, source_target_pairs={{0,3},{1,2},{2,5},{3,4},{4,7},{5,6},{6,1},{7,0},{8,11},{9,10},{10,... | collective-permute-start | bytes 393224 | tf_op jit(solution)/shard_map/ppermute | solution.py:216
  68.2 3.0 %collective-permute-start.10 = (bf16[64,1024]{1,0:T(8,128)(2,1)S(1)}, bf16[64,1024]{1,0:T(8,128)(2,1)S(1)}, u32[]{:S(2)}, u32[]{:S(2)}) collective-permute-start(bf16[64,1024]{1,0:T(8,128)(2,1)S(1)} %get-tuple-element.34), channel_id=1, source_target_pairs={{0,7},{1,6},{2,1},{3,0},{4,3},{5,2},{6,5},{7,4},{8,15},{9,14},{10,... | collective-permute-start | bytes 393224 | tf_op jit(solution)/shard_map/ppermute | solution.py:216
  71.2 2.0 %collective-permute-start.11 = (bf16[64,1024]{1,0:T(8,128)(2,1)S(1)}, bf16[64,1024]{1,0:T(8,128)(2,1)S(1)}, u32[]{:S(2)}, u32[]{:S(2)}) collective-permute-start(bf16[64,1024]{1,0:T(8,128)(2,1)S(1)} %get-tuple-element.35), channel_id=1, source_target_pairs={{0,4},{1,5},{2,6},{3,7},{4,0},{5,1},{6,2},{7,3},{8,12},{9,13},{10,... | collective-permute-start | bytes 393224 | tf_op jit(solution)/shard_map/ppermute | solution.py:216
  73.2 2.1 %collective-permute-done.8.refs_3_ = bf16[64,1024]{1,0:T(8,128)(2,1)S(1)} collective-permute-done((bf16[64,1024]{1,0:T(8,128)(2,1)S(1)}, bf16[64,1024]{1,0:T(8,128)(2,1)S(1)}, u32[]{:S(2)}, u32[]{:S(2)}) %collective-permute-start.8) | collective-permute-done | bytes 131104 | tf_op jit(solution)/shard_map/ppermute | solution.py:216
  75.2 0.9 %collective-permute-done.9.refs_4_ = bf16[64,1024]{1,0:T(8,128)(2,1)S(1)} collective-permute-done((bf16[64,1024]{1,0:T(8,128)(2,1)S(1)}, bf16[64,1024]{1,0:T(8,128)(2,1)S(1)}, u32[]{:S(2)}, u32[]{:S(2)}) %collective-permute-start.9) | collective-permute-done | bytes 131104 | tf_op jit(solution)/shard_map/ppermute | solution.py:216
  76.2 1.9 %collective-permute-done.11.refs_6_ = bf16[64,1024]{1,0:T(8,128)(2,1)S(1)} collective-permute-done((bf16[64,1024]{1,0:T(8,128)(2,1)S(1)}, bf16[64,1024]{1,0:T(8,128)(2,1)S(1)}, u32[]{:S(2)}, u32[]{:S(2)}) %collective-permute-start.11) | collective-permute-done | bytes 131104 | tf_op jit(solution)/shard_map/ppermute | solution.py:216
  78.1 0.9 %finish.1 = bf16[60,4096]{1,0:T(8,128)(2,1)} custom-call(bf16[64,1024]{1,0:T(8,128)(2,1)S(1)} %collective-permute-done.5.refs_0_, bf16[64,1024]{1,0:T(8,128)(2,1)S(1)} %collective-permute-done.6.refs_1_, bf16[64,1024]{1,0:T(8,128)(2,1)S(1)} %collective-permute-done.7.refs_2_, bf16[64,1024]{1,0:T(8,128)(2,1)S(1)} %collective-permute-done.8.refs_3_, ...), custom_call_target="tpu_custom_call" | custom-call | tf_op jit(solution)/shard_map/finish/pallas_call | solution.py:199
  (15 shorter events, 0.2 us)
Async XLA Ops:
  0.0 2.8 %copy-start.1 = (f32[64,256]{1,0:T(8,128)S(1)}, f32[64,256]{1,0:T(8,128)}, u32[]{:S(2)}) copy-start(f32[64,256]{1,0:T(8,128)} %phases.1) | copy-start | bytes 196612
  0.0 2.8 %copy-start.2 = (s32[4096]{0:T(1024)S(1)}, s32[4096]{0:T(1024)}, u32[]{:S(2)}) copy-start(s32[4096]{0:T(1024)} %param.9) | copy-start | bytes 49156
  2.8 15.9 %copy-start = (bf16[2,480,480]{2,1,0:T(8,128)(2,1)S(1)}, bf16[2,480,480]{2,1,0:T(8,128)(2,1)}, u32[]{:S(2)}) copy-start(bf16[2,480,480]{2,1,0:T(8,128)(2,1)} %tables.1) | copy-start | bytes 2764804
  4.5 1.4 %collective-permute-start = (bf16[128,480]{1,0:T(8,128)(2,1)S(1)}, bf16[128,480]{1,0:T(8,128)(2,1)S(1)}, u32[]{:S(2)}, u32[]{:S(2)}) collective-permute-start(bf16[128,480]{1,0:T(8,128)(2,1)S(1)} %get-tuple-element.27), channel_id=1, source_target_pairs={{0,8},{8,0},{1,9},{9,1},{2,10},{10,2},{3,11},{11,3},{4,12},{12,4},... | collective-permute-start | bytes 368648 | tf_op jit(solution)/shard_map/ppermute | solution.py:243
  19.9 16.7 %all-to-all-start.1 = ((bf16[32,16,512]{2,1,0:T(8,128)(2,1)}), bf16[32,16,512]{2,1,0:T(8,128)(2,1)S(1)}, u32[]{:S(2)}, u32[]{:S(2)}) async-start(bf16[32,16,512]{2,1,0:T(8,128)(2,1)} %angular.1), calls=%async_computation.1 | async-start | bytes 1048576 | tf_op jit(solution)/shard_map/all_to_all | solution.py:228
  25.6 20.4 %collective-permute-start.2 = (bf16[1024,256]{1,0:T(8,128)(2,1)S(1)}, bf16[1024,256]{1,0:T(8,128)(2,1)S(1)}, u32[]{:S(2)}, u32[]{:S(2)}) collective-permute-start(bf16[1024,256]{1,0:T(8,128)(2,1)S(1)} %get-tuple-element.21.p1), channel_id=1, source_target_pairs={{0,2},{2,4},{4,6},{6,0},{1,3},{3,5},{5,7},{7,1},{8,10},{10,12},{12... | collective-permute-start | bytes 1572872 | tf_op jit(solution)/shard_map/ppermute | solution.py:245
  27.5 28.9 %collective-permute-start.3 = (bf16[1024,256]{1,0:T(8,128)(2,1)S(1)}, bf16[1024,256]{1,0:T(8,128)(2,1)}, u32[]{:S(2)}, u32[]{:S(2)}) collective-permute-start(bf16[1024,256]{1,0:T(8,128)(2,1)S(1)} %get-tuple-element.22.p2), channel_id=1, source_target_pairs={{0,4},{2,6},{4,0},{6,2},{1,5},{3,7},{5,1},{7,3},{8,12},{10,14},{12... | collective-permute-start | bytes 1572872 | tf_op jit(solution)/shard_map/ppermute | solution.py:245
  30.2 26.1 %collective-permute-start.4 = (bf16[1024,256]{1,0:T(8,128)(2,1)S(1)}, bf16[1024,256]{1,0:T(8,128)(2,1)}, u32[]{:S(2)}, u32[]{:S(2)}) collective-permute-start(bf16[1024,256]{1,0:T(8,128)(2,1)S(1)} %get-tuple-element.23.p3), channel_id=1, source_target_pairs={{0,6},{2,0},{4,2},{6,4},{1,7},{3,1},{5,3},{7,5},{8,14},{10,8},{12,... | collective-permute-start | bytes 1572872 | tf_op jit(solution)/shard_map/ppermute | solution.py:245
  36.6 19.7 %collective-permute-start.1 = (bf16[4,128,512]{2,1,0:T(8,128)(2,1)S(1)}, bf16[4,128,512]{2,1,0:T(8,128)(2,1)S(1)}, u32[]{:S(2)}, u32[]{:S(2)}) collective-permute-start(bf16[4,128,512]{2,1,0:T(8,128)(2,1)S(1)} %bitcast.5), channel_id=1, source_target_pairs={{0,8},{8,0},{1,9},{9,1},{2,10},{10,2},{3,11},{11,3},{4,12},{12,4},... | collective-permute-start | bytes 1572872 | tf_op jit(solution)/shard_map/ppermute | solution.py:253
  58.9 9.3 %collective-permute-start.5 = (bf16[64,1024]{1,0:T(8,128)(2,1)S(1)}, bf16[64,1024]{1,0:T(8,128)(2,1)S(1)}, u32[]{:S(2)}, u32[]{:S(2)}) collective-permute-start(bf16[64,1024]{1,0:T(8,128)(2,1)S(1)} %get-tuple-element.29), channel_id=1, source_target_pairs={{0,1},{1,0},{2,3},{3,2},{4,5},{5,4},{6,7},{7,6},{8,9},{9,8},{10,11... | collective-permute-start | bytes 393224 | tf_op jit(solution)/shard_map/ppermute | solution.py:216
  61.7 9.5 %collective-permute-start.6 = (bf16[64,1024]{1,0:T(8,128)(2,1)S(1)}, bf16[64,1024]{1,0:T(8,128)(2,1)S(1)}, u32[]{:S(2)}, u32[]{:S(2)}) collective-permute-start(bf16[64,1024]{1,0:T(8,128)(2,1)S(1)} %get-tuple-element.30), channel_id=1, source_target_pairs={{0,2},{1,3},{2,4},{3,5},{4,6},{5,7},{6,0},{7,1},{8,10},{9,11},{10,... | collective-permute-start | bytes 393224 | tf_op jit(solution)/shard_map/ppermute | solution.py:216
  62.2 10.9 %collective-permute-start.7 = (bf16[64,1024]{1,0:T(8,128)(2,1)S(1)}, bf16[64,1024]{1,0:T(8,128)(2,1)S(1)}, u32[]{:S(2)}, u32[]{:S(2)}) collective-permute-start(bf16[64,1024]{1,0:T(8,128)(2,1)S(1)} %get-tuple-element.31), channel_id=1, source_target_pairs={{0,6},{1,7},{2,0},{3,1},{4,2},{5,3},{6,4},{7,5},{8,14},{9,15},{10,... | collective-permute-start | bytes 393224 | tf_op jit(solution)/shard_map/ppermute | solution.py:216
  65.0 10.3 %collective-permute-start.8 = (bf16[64,1024]{1,0:T(8,128)(2,1)S(1)}, bf16[64,1024]{1,0:T(8,128)(2,1)S(1)}, u32[]{:S(2)}, u32[]{:S(2)}) collective-permute-start(bf16[64,1024]{1,0:T(8,128)(2,1)S(1)} %get-tuple-element.32), channel_id=1, source_target_pairs={{0,5},{1,4},{2,7},{3,6},{4,1},{5,0},{6,3},{7,2},{8,13},{9,12},{10,... | collective-permute-start | bytes 393224 | tf_op jit(solution)/shard_map/ppermute | solution.py:216
  65.6 10.6 %collective-permute-start.9 = (bf16[64,1024]{1,0:T(8,128)(2,1)S(1)}, bf16[64,1024]{1,0:T(8,128)(2,1)S(1)}, u32[]{:S(2)}, u32[]{:S(2)}) collective-permute-start(bf16[64,1024]{1,0:T(8,128)(2,1)S(1)} %get-tuple-element.33), channel_id=1, source_target_pairs={{0,3},{1,2},{2,5},{3,4},{4,7},{5,6},{6,1},{7,0},{8,11},{9,10},{10,... | collective-permute-start | bytes 393224 | tf_op jit(solution)/shard_map/ppermute | solution.py:216
  68.2 8.0 %collective-permute-start.10 = (bf16[64,1024]{1,0:T(8,128)(2,1)S(1)}, bf16[64,1024]{1,0:T(8,128)(2,1)S(1)}, u32[]{:S(2)}, u32[]{:S(2)}) collective-permute-start(bf16[64,1024]{1,0:T(8,128)(2,1)S(1)} %get-tuple-element.34), channel_id=1, source_target_pairs={{0,7},{1,6},{2,1},{3,0},{4,3},{5,2},{6,5},{7,4},{8,15},{9,14},{10,... | collective-permute-start | bytes 393224 | tf_op jit(solution)/shard_map/ppermute | solution.py:216
  71.2 6.9 %collective-permute-start.11 = (bf16[64,1024]{1,0:T(8,128)(2,1)S(1)}, bf16[64,1024]{1,0:T(8,128)(2,1)S(1)}, u32[]{:S(2)}, u32[]{:S(2)}) collective-permute-start(bf16[64,1024]{1,0:T(8,128)(2,1)S(1)} %get-tuple-element.35), channel_id=1, source_target_pairs={{0,4},{1,5},{2,6},{3,7},{4,0},{5,1},{6,2},{7,3},{8,12},{9,13},{10,... | collective-permute-start | bytes 393224 | tf_op jit(solution)/shard_map/ppermute | solution.py:216
